TPU v7x, 32 devices: a whole 2x2x4 slice. The times are simulated.
32 devices in a mesh: slab: 8 (over y, x, core), cross: 4 (over z).
Axes of the slice: x: 2, y: 2, z: 4, core: 2. Of those that a mesh axis runs over, the one named last changes fastest.
Arguments:
- velocity: float32 [3, 32, 64, 128], P(None, 'slab', 'cross'), may hold values from -6 to 6
- density: float32 [32, 64, 128], P('slab', 'cross'), may hold values from 0.5 to 2
- source: float32 [32, 64, 128], P('slab', 'cross'), may hold values from -6 to 6
- species: float32 [9, 32, 64, 128], P(None, 'slab', 'cross'), may hold values from 0 to 1
Outputs:
- velocity_out: float32 [3, 32, 64, 128], P(None, 'slab', 'cross')
- pressure: float32 [32, 64, 128], P('slab', 'cross')
- species_out: float32 [9, 32, 64, 128], P(None, 'slab', 'cross')
All inputs are finite; a program needn't handle non-finite values.
Results may differ from a plain program's by a relative error of at most 0.0001.
Values sent between devices are 32-bit elements; how exact they have to be, the bound alone decides.
A program may use at most 64 MiB of HBM per device.

v0:
```python
import functools

import jax
import jax.numpy as jnp
from jax import lax
from jax.experimental import pallas as pl
from jax.experimental.pallas import tpu as pltpu
from jax.sharding import PartitionSpec as P

CYCLES = 2
COARSE = 4
damping = 0.8
time_step = 0.25
MESH = pl.DeviceIdType.MESH
RX = 5
RY = 8
CX = 6
CY = 12

NEAR = [(dx, dy) for dx in (-1, 0, 1) for dy in (-1, 0, 1) if (dx, dy) != (0, 0)] + [(-2, 0), (2, 0)]
WIDE = [(dx, dy) for dx in range(-3, 4) for dy in (-1, 0, 1) if (dx, dy) != (0, 0)]
SIDE = [(-1, 0), (1, 0), (0, -1), (0, 1)]
HX, HY = RX, RY


def kernel(
    slabs, crosses, velocity_in, density_in, source_in, species,
    out_x, out_y, out_z, out_p, rim_x, rim_y,
    velocity, density, source, fields, packed_m, packed_r, press, coarse_m, right,
    xa, xb, ya, yb, za, zb, goal, scale_back, pa, pb,
    cxa, cxb, cya, cyb, cza, czb, cinv, ca, cb, in_sem,
    f_send, f_recv, m_send, m_recv, r_send, r_recv, p_send, p_recv, s_send, s_recv,
):
    cells_x, cells_y, cells_z = density.shape
    wx, wy = cells_x + 2 * HX, cells_y + 2 * HY
    half = cells_x // 2
    cw, cy = half + 2 * CX, cells_y + 2 * CY
    own_y = pl.ds(HY, cells_y)
    own_x = pl.ds(HX, cells_x)
    own_cy = pl.ds(CY, cells_y)
    slab, cross = lax.axis_index("slab"), lax.axis_index("cross")
    f32 = jnp.float32

    def there(dx, dy):
        return (slab + dx >= 0) & (slab + dx < slabs) & (cross + dy >= 0) & (cross + dy < crosses)

    def ys(dy, k, rim):
        if dy == 0:
            return pl.ds(rim, cells_y), pl.ds(rim, cells_y)
        if dy > 0:
            return pl.ds(rim + cells_y - k, k), pl.ds(rim - k, k)
        return pl.ds(rim, k), pl.ds(rim + cells_y, k)

    def fine_cut(dx, dy):
        step = max(0, (abs(dx) - 1) * cells_x + 1) if dx != 0 else 0
        k = RX - step
        sy, dyy = ys(dy, k, HY)
        depth = min(cells_x, RX + 1 - step) if dx != 0 else cells_x
        if dx == 0:
            sx, dst_x = own_x, own_x
        elif dx > 0:
            sx, dst_x = pl.ds(HX + cells_x - depth, depth), pl.ds(HX + (1 - dx) * cells_x - depth, depth)
        else:
            sx, dst_x = pl.ds(HX, depth), pl.ds(HX - dx * cells_x, depth)
        return (sx, sy), (dst_x, dyy)

    def coarse_cut(dx, dy):
        step = (abs(dx) - 1) * half + 1 if dx != 0 else 0
        sy, dyy = ys(dy, 2 * (CX - step), CY)
        return (CX // half, sy), (CX // half - dx, dyy)

    def within(cut, ref, *lead):
        def both(dx, dy):
            src, dst = cut(dx, dy)
            return ref.at[lead + src], ref.at[lead + dst]

        return both

    def exchange(directions, cut, send, recv):
        def copy(index, dx, dy):
            src, dst = cut(dx, dy)
            return pltpu.make_async_remote_copy(
                src_ref=src, dst_ref=dst, send_sem=send.at[index], recv_sem=recv.at[index],
                device_id=(slab + dx, cross + dy), device_id_type=MESH,
            )

        def start():
            for index, (dx, dy) in enumerate(directions):
                @pl.when(there(dx, dy))
                def _():
                    copy(index, dx, dy).start()

        def arrive():
            for index, (dx, dy) in enumerate(directions):
                @pl.when(there(-dx, -dy))
                def _():
                    copy(index, dx, dy).wait_recv()

        def leave():
            for index, (dx, dy) in enumerate(directions):
                @pl.when(there(dx, dy))
                def _():
                    copy(index, dx, dy).wait_send()

        return start, arrive, leave

    def fields_cut(dx, dy):
        return within(fine_cut, fields, slice(0, 2) if abs(dx) > 1 else slice(None))(dx, dy)

    f_x = exchange(NEAR, fields_cut, f_send, f_recv)
    m_x = exchange(WIDE, within(coarse_cut, packed_m), m_send, m_recv)
    r_x = [exchange(WIDE, within(coarse_cut, packed_r, at), r_send.at[at], r_recv.at[at]) for at in range(CYCLES)]
    p_x = [exchange(NEAR, within(fine_cut, press, at), p_send.at[at], p_recv.at[at]) for at in range(CYCLES)]

    def species_cut(dx, dy):
        if dx != 0:
            return species.at[:, cells_x - 1 if dx > 0 else 0], rim_x.at[0 if dx > 0 else 1]
        return species.at[:, :, cells_y - 1 if dy > 0 else 0], rim_y.at[0 if dy > 0 else 1]

    s_x = exchange(SIDE, species_cut, s_send, s_recv)

    def grids(rows):
        lane = lax.broadcasted_iota(jnp.int32, (rows, cells_z), 1)
        row = lax.broadcasted_iota(jnp.int32, (rows, cells_z), 0)
        return row, lane

    def next_z(v, k=1):
        return pltpu.roll(v, cells_z - k, 1)

    def prev_z(v, k=1):
        return pltpu.roll(v, k, 1)

    def next_y(v, k=1):
        return pltpu.roll(v, v.shape[0] - k, 0)

    def prev_y(v, k=1):
        return pltpu.roll(v, k, 0)

    row_w, lane_w = grids(wy)
    row_c, lane_c = grids(cy)
    row_o, lane_o = grids(cells_y)

    def pair_sum(v, row, lane):
        v = v + jnp.where(row % 2 == 0, next_y(v), prev_y(v))
        return v + jnp.where(lane % 2 == 0, next_z(v), prev_z(v))

    def pack(two):
        return jnp.where(lane_o % 2 == 0, two[0], two[1])

    def unpack(ref, dst):
        for block in range(2 * CX // half + 1):
            e = ref[block]
            dst[2 * block] = jnp.where(lane_c % 2 == 0, e, prev_z(e))
            dst[2 * block + 1] = jnp.where(lane_c % 2 == 0, next_z(e), e)

    inputs = [
        pltpu.make_async_copy(src, dst, in_sem.at[at])
        for at, (src, dst) in enumerate(((velocity_in, velocity), (density_in, density), (source_in, source)))
    ]
    for copy in inputs:
        copy.start()
    for ref in (fields, packed_m, packed_r, press, rim_x, rim_y):
        ref[...] = jnp.zeros(ref.shape, f32)
    barrier = pltpu.get_barrier_semaphore()
    count = jnp.int32(0)
    for dx, dy in WIDE:
        here = there(dx, dy)
        count = count + here.astype(jnp.int32)

        @pl.when(here)
        def _():
            pl.semaphore_signal(barrier, inc=1, device_id=(slab + dx, cross + dy), device_id_type=MESH)

    for copy in inputs:
        copy.wait()
    for x in range(cells_x):
        v2 = velocity[2, x]
        dz = jnp.where(lane_o == cells_z - 1, 0.0, next_z(v2)) - jnp.where(lane_o == 0, 0.0, prev_z(v2))
        fields[0, HX + x, own_y] = 1.0 / density[x]
        fields[1, HX + x, own_y] = velocity[0, x]
        fields[2, HX + x, own_y] = velocity[1, x]
        fields[3, HX + x, own_y] = 0.5 * dz - source[x]
    means = []
    for c in range(half):
        m = 1.0 / density[2 * c] + 1.0 / density[2 * c + 1]
        means.append(0.125 * pair_sum(m, row_o, lane_o))
    packed_m[CX // half, own_cy] = pack(means)
    pl.semaphore_wait(barrier, count)
    f_x[0]()
    m_x[0]()
    s_x[0]()
    f_x[1]()

    def fine_setup(rows):
        for x in rows:
            m = fields[0, x]
            lo_x, hi_x = 0.5 * (m + fields[0, x - 1]), 0.5 * (m + fields[0, x + 1])
            lo_y, hi_y = 0.5 * (m + prev_y(m)), 0.5 * (m + next_y(m))
            lo_z = 0.5 * (m + jnp.where(lane_w == 0, 0.0, prev_z(m)))
            hi_z = 0.5 * (m + jnp.where(lane_w == cells_z - 1, 0.0, next_z(m)))
            diag = lo_x + hi_x + lo_y + hi_y + lo_z + hi_z
            inside = m > 0.0
            inv = jnp.where(inside, damping / jnp.where(inside, diag, 1.0), 0.0)
            xa[x], xb[x] = lo_x * inv, hi_x * inv
            ya[x], yb[x] = lo_y * inv, hi_y * inv
            za[x] = jnp.where(lane_w == 0, 0.0, lo_z * inv)
            zb[x] = jnp.where(lane_w == cells_z - 1, 0.0, hi_z * inv)
            if HX <= x < HX + cells_x:
                scale_back[x - HX] = (diag * (1.0 / damping))[HY : HY + cells_y]
            v1 = fields[2, x]
            t = 0.5 * ((fields[1, x + 1] - fields[1, x - 1]) + (next_y(v1) - prev_y(v1))) + fields[3, x]
            b = t * inv
            goal[x] = b
            pa[x] = -b

    early = range(HX - 2, HX + cells_x + 2)
    fine_setup(early)

    def sweep(src, dst, coefs, right, low, high, k):
        xl, xu, yl, yu, zl, zu = coefs
        for x in range(low, high):
            v = src[x]
            t = xl[x] * src[x - 1] + xu[x] * src[x + 1]
            t = t + (yl[x] * prev_y(v, k) + yu[x] * next_y(v, k))
            t = t + (zl[x] * prev_z(v, k) + zu[x] * next_z(v, k))
            dst[x] = (1.0 - damping) * v + (t - right[x])

    fine = (xa, xb, ya, yb, za, zb)
    coarse = (cxa, cxb, cya, cyb, cza, czb)

    def coarse_setup(rows):
        for x in rows:
            m = coarse_m[x]
            lo_x, hi_x = 0.5 * (m + coarse_m[x - 1]), 0.5 * (m + coarse_m[x + 1])
            lo_y, hi_y = 0.5 * (m + prev_y(m, 2)), 0.5 * (m + next_y(m, 2))
            lo_z = 0.5 * (m + jnp.where(lane_c < 2, 0.0, prev_z(m, 2)))
            hi_z = 0.5 * (m + jnp.where(lane_c >= cells_z - 2, 0.0, next_z(m, 2)))
            diag = lo_x + hi_x + lo_y + hi_y + lo_z + hi_z
            inside = m > 0.0
            inv = jnp.where(inside, damping / jnp.where(inside, diag, 1.0), 0.0)
            cxa[x], cxb[x] = lo_x * inv, hi_x * inv
            cya[x], cyb[x] = lo_y * inv, hi_y * inv
            cza[x] = jnp.where(lane_c < 2, 0.0, lo_z * inv)
            czb[x] = jnp.where(lane_c >= cells_z - 2, 0.0, hi_z * inv)
            if CX <= x < CX + half:
                cinv[x - CX] = inv[CY : CY + cells_y]

    def correct(at, pre, free, reach):
        for x in range(HX, HX + cells_x):
            press[at, x, own_y] = pre[x, own_y]
        own_rows = range(CX, CX + half)
        if at == 0:
            m_x[1]()
            unpack(packed_m, coarse_m)
            coarse_setup(own_rows)
        sums = []
        for c in range(half):
            r = None
            for x in (HX + 2 * c, HX + 2 * c + 1):
                v = pre[x]
                t = xa[x] * pre[x - 1] + xb[x] * pre[x + 1]
                t = t + (ya[x] * prev_y(v) + yb[x] * next_y(v))
                t = t + (za[x] * prev_z(v) + zb[x] * next_z(v))
                d = (damping * v - (t - goal[x]))[HY : HY + cells_y] * scale_back[x - HX]
                r = d if r is None else r + d
            sums.append(0.5 * pair_sum(r, row_o, lane_o) * cinv[c])
        packed_r[at, CX // half, own_cy] = pack(sums)
        r_x[at][0]()
        p_x[at][0]()
        if at == 0:
            coarse_setup([x for x in range(1, cw - 1) if x not in own_rows])
            fine_setup([x for x in range(1, wx - 1) if x not in early])
        r_x[at][1]()
        unpack(packed_r.at[at], right)
        for x in range(cw):
            ca[x] = -right[x]
        src, dst = ca, cb
        for step in range(1, COARSE):
            sweep(src, dst, coarse, right, step, cw - step, 2)
            src, dst = dst, src
        p_x[at][1]()
        low, high = HX - reach - 2, HX + cells_x + reach + 2
        for x in range(low, high):
            pre[x] = press[at, x] + src[CX + (x - HX) // 2, pl.ds(CY - HY, wy)]
        sweep(pre, free, fine, goal, low + 1, high - 1, 1)
        sweep(free, pre, fine, goal, low + 2, high - 2, 1)

    sweep(pa, pb, fine, goal, HX - 1, HX + cells_x + 1, 1)
    correct(0, pb, pa, 3)
    sweep(pb, pa, fine, goal, HX - 2, HX + cells_x + 2, 1)
    sweep(pa, pb, fine, goal, HX - 1, HX + cells_x + 1, 1)
    correct(1, pb, pa, 2)
    last = pb

    for x in range(HX - 1, HX + cells_x + 1):
        grad = 0.5 * (last[x + 1, own_y] - last[x - 1, own_y])
        out_x[x - HX + 1] = fields[1, x, own_y] - fields[0, x, own_y] * grad
    for x in range(cells_x):
        w = x + HX
        v = last[w]
        out_y[x] = fields[2, w] - fields[0, w] * (0.5 * (next_y(v) - prev_y(v)))
        own = v[HY : HY + cells_y]
        dz = jnp.where(lane_o == cells_z - 1, 0.0, next_z(own)) - jnp.where(lane_o == 0, 0.0, prev_z(own))
        out_z[x] = velocity[2, x] - fields[0, w, own_y] * (0.5 * dz)
        out_p[x] = own
    s_x[1]()
    for x in (f_x, m_x, s_x, *r_x, *p_x):
        x[2]()


def transport(in_x, in_y, in_z, in_p, rim_x, rim_y, species, vel_out, pres_out, spec_out):
    cells_x, cells_y, cells_z = in_p.shape
    lane_o = lax.broadcasted_iota(jnp.int32, (cells_y, cells_z), 1)
    row_o = lax.broadcasted_iota(jnp.int32, (cells_y, cells_z), 0)

    def next_z(v):
        return pltpu.roll(v, cells_z - 1, 1)

    def prev_z(v):
        return pltpu.roll(v, 1, 1)

    def next_y(v):
        return pltpu.roll(v, v.shape[0] - 1, 0)

    def prev_y(v):
        return pltpu.roll(v, 1, 0)

    mid = slice(HY, HY + cells_y)
    pres_out[...] = in_p[...]
    move_x = [in_x[x] for x in range(cells_x + 2)]
    for x in range(cells_x):
        move_y, move_z = in_y[x], in_z[x]
        vel_out[0, x] = move_x[x + 1]
        vel_out[1, x] = move_y[mid]
        vel_out[2, x] = move_z
        lo_x, hi_x = 0.5 * (move_x[x] + move_x[x + 1]), 0.5 * (move_x[x + 1] + move_x[x + 2])
        lo_y, hi_y = (0.5 * (move_y + prev_y(move_y)))[mid], (0.5 * (move_y + next_y(move_y)))[mid]
        lo_z = 0.5 * (move_z + jnp.where(lane_o == 0, 0.0, prev_z(move_z)))
        hi_z = 0.5 * (move_z + jnp.where(lane_o == cells_z - 1, 0.0, next_z(move_z)))

        def into(flow):
            return time_step * jnp.maximum(flow, 0.0)

        def back(flow):
            return -time_step * jnp.minimum(flow, 0.0)

        keep = 1.0 - (into(hi_x) + into(hi_y) + into(hi_z)) - (back(lo_x) + back(lo_y) + back(lo_z))
        from_xl, from_xu = into(lo_x), back(hi_x)
        from_yl, from_yu = into(lo_y), back(hi_y)
        from_zl = jnp.where(lane_o == 0, 0.0, into(lo_z))
        from_zu = jnp.where(lane_o == cells_z - 1, 0.0, back(hi_z))
        for s in range(species.shape[0]):
            q = species[s, x]
            xl = rim_x[0, s] if x == 0 else species[s, x - 1]
            xu = rim_x[1, s] if x == cells_x - 1 else species[s, x + 1]
            yl = jnp.where(row_o == 0, rim_y[0, s, pl.ds(x, 1)], prev_y(q))
            yu = jnp.where(row_o == cells_y - 1, rim_y[1, s, pl.ds(x, 1)], next_y(q))
            total = keep * q + (from_xl * xl + from_xu * xu) + (from_yl * yl + from_yu * yu)
            spec_out[s, x] = total + (from_zl * prev_z(q) + from_zu * next_z(q))


def local(slabs, crosses, velocity, density, source, species):
    cells_x, cells_y, cells_z = density.shape
    assert cells_x == 4 and CX % (cells_x // 2) == 0 and cells_y % 8 == 0 and cells_y >= CY
    wx, wy = cells_x + 2 * HX, cells_y + 2 * HY
    half = cells_x // 2
    kinds = species.shape[0]
    f32 = jnp.float32

    def vmem(*shape):
        return pltpu.VMEM(shape, f32)

    fine, coarse = (wx, wy, cells_z), (half + 2 * CX, cells_y + 2 * CY, cells_z)
    packed = (2 * CX // half + 1,) + coarse[1:]
    near, wide, side = len(NEAR), len(WIDE), len(SIDE)
    dma = pltpu.SemaphoreType.DMA
    spec = pl.BlockSpec(memory_space=pltpu.VMEM)
    anywhere = pl.BlockSpec(memory_space=pl.ANY)
    moved = [
        (cells_x + 2, cells_y, cells_z), (cells_x, wy, cells_z), density.shape, density.shape,
        (2, kinds, cells_y, cells_z), (2, kinds, cells_x, cells_z),
    ]
    between = pl.pallas_call(
        functools.partial(kernel, slabs, crosses),
        out_shape=tuple(jax.ShapeDtypeStruct(shape, f32) for shape in moved),
        in_specs=[anywhere] * 4,
        out_specs=(spec,) * 6,
        scratch_shapes=[vmem(*velocity.shape), vmem(*density.shape), vmem(*density.shape)]
        + [vmem(4, *fine), vmem(*packed), vmem(CYCLES, *packed), vmem(CYCLES, *fine)]
        + [vmem(*coarse)] * 2
        + [vmem(*fine)] * 7 + [vmem(*density.shape)] + [vmem(*fine)] * 2
        + [vmem(*coarse)] * 6 + [vmem(half, cells_y, cells_z)] + [vmem(*coarse)] * 2
        + [dma((3,))] + [dma((near,))] * 2 + [dma((wide,))] * 2
        + [dma((CYCLES, wide))] * 2 + [dma((CYCLES, near))] * 2 + [dma((side,))] * 2,
        compiler_params=pltpu.CompilerParams(collective_id=0, has_side_effects=True),
        name="projection",
    )(velocity, density, source, species)
    return pl.pallas_call(
        transport,
        out_shape=tuple(jax.ShapeDtypeStruct(a.shape, f32) for a in (velocity, density, species)),
        in_specs=[spec] * 7,
        out_specs=(spec,) * 3,
        name="transport",
    )(*between, species)


def solution(mesh):
    plane, stack = P("slab", "cross", None), P(None, "slab", "cross", None)
    return jax.shard_map(
        functools.partial(local, mesh.shape["slab"], mesh.shape["cross"]),
        mesh=mesh,
        in_specs=(stack, plane, plane, stack),
        out_specs=(stack, plane, stack),
        check_vma=False,
    )
```

profile of v0, /device:TPU:0, one launch (start us, length us, event | category | flops | bytes accessed | tf_op | source)
XLA Modules:
  0.0 28.8 jit_solution(10334221446103131715)
XLA Ops:
  0.6 25.9 %projection.1 = (f32[6,16,128]{2,1,0:T(8,128)}, f32[4,32,128]{2,1,0:T(8,128)}, f32[4,16,128]{2,1,0:T(8,128)}, f32[4,16,128]{2,1,0:T(8,128)}, f32[2,9,16,128]{3,2,1,0:T(8,128)}, /*index=5*/f32[2,9,4,128]{3,2,1,0:T(4,128)}) custom-call(f32[3,4,16,128]{3,2,1,0:T(8,128)} %velocity_in.1, f32[4,16,128]{2,1,0:T(8,128)} %density_in.1, f32[4,16,128]{2,1,0:T(8,128)} %source_in.1, ...), custom_call_target="tpu_custom_call" | custom-call | tf_op jit(solution)/shard_map/projection/pallas_call | solution.py:383
  26.6 2.2 %transport.1 = (f32[3,4,16,128]{3,2,1,0:T(8,128)}, f32[4,16,128]{2,1,0:T(8,128)}, f32[9,4,16,128]{3,2,1,0:T(8,128)}) custom-call(f32[6,16,128]{2,1,0:T(8,128)} %get-tuple-element.9.in_x, f32[4,32,128]{2,1,0:T(8,128)} %get-tuple-element.10.in_y, f32[4,16,128]{2,1,0:T(8,128)} %get-tuple-element.11.in_z, f32[4,16,128]{2,1,0:T(8,128)} %get-tuple-element.12.in_p, ...), custom_call_target="tpu_custom_call" | custom-call | tf_op jit(solution)/shard_map/transport/pallas_call | solution.py:398
where the time goes:
time: 28.9 us; the launch traced here: 28.8 us
  Pallas kernels  28.1 us (97%)
  between operations  0.64 us (2%)
    pallas_call x1, Pallas kernels, local(): pl.pallas_call(functools.partial(kernel, slabs, crosses), out_shape=tuple...  25.9 us
    pallas_call x1, Pallas kernels, local(): pl.pallas_call(transport, out_shape=tuple((jax.ShapeDtypeStruct(a.shape,...  2.17 us

commit v1 on v0

--- a/solution.py
+++ b/solution.py
@@ -25,7 +25,7 @@
 
 def kernel(
     slabs, crosses, velocity_in, density_in, source_in, species,
-    out_x, out_y, out_z, out_p, rim_x, rim_y,
+    out_x, out_y, out_z, out_p, rim_x, rim_y, kinds,
     velocity, density, source, fields, packed_m, packed_r, press, coarse_m, right,
     xa, xb, ya, yb, za, zb, goal, scale_back, pa, pb,
     cxa, cxb, cya, cyb, cza, czb, cinv, ca, cb, in_sem,
@@ -114,8 +114,8 @@
 
     def species_cut(dx, dy):
         if dx != 0:
-            return species.at[:, cells_x - 1 if dx > 0 else 0], rim_x.at[0 if dx > 0 else 1]
-        return species.at[:, :, cells_y - 1 if dy > 0 else 0], rim_y.at[0 if dy > 0 else 1]
+            return kinds.at[:, cells_x - 1 if dx > 0 else 0], rim_x.at[0 if dx > 0 else 1]
+        return kinds.at[:, :, cells_y - 1 if dy > 0 else 0], rim_y.at[0 if dy > 0 else 1]
 
     s_x = exchange(SIDE, species_cut, s_send, s_recv)
 
@@ -155,7 +155,9 @@
 
     inputs = [
         pltpu.make_async_copy(src, dst, in_sem.at[at])
-        for at, (src, dst) in enumerate(((velocity_in, velocity), (density_in, density), (source_in, source)))
+        for at, (src, dst) in enumerate(
+            ((velocity_in, velocity), (density_in, density), (source_in, source), (species, kinds))
+        )
     ]
     for copy in inputs:
         copy.start()
@@ -171,7 +173,7 @@
         def _():
             pl.semaphore_signal(barrier, inc=1, device_id=(slab + dx, cross + dy), device_id_type=MESH)
 
-    for copy in inputs:
+    for copy in inputs[:3]:
         copy.wait()
     for x in range(cells_x):
         v2 = velocity[2, x]
@@ -188,6 +190,7 @@
     pl.semaphore_wait(barrier, count)
     f_x[0]()
     m_x[0]()
+    inputs[3].wait()
     s_x[0]()
     f_x[1]()
 
@@ -375,33 +378,36 @@
     near, wide, side = len(NEAR), len(WIDE), len(SIDE)
     dma = pltpu.SemaphoreType.DMA
     spec = pl.BlockSpec(memory_space=pltpu.VMEM)
-    anywhere = pl.BlockSpec(memory_space=pl.ANY)
+    far = pl.BlockSpec(memory_space=pltpu.HBM)
     moved = [
         (cells_x + 2, cells_y, cells_z), (cells_x, wy, cells_z), density.shape, density.shape,
-        (2, kinds, cells_y, cells_z), (2, kinds, cells_x, cells_z),
+        (2, kinds, cells_y, cells_z), (2, kinds, cells_x, cells_z), species.shape,
     ]
     between = pl.pallas_call(
         functools.partial(kernel, slabs, crosses),
-        out_shape=tuple(jax.ShapeDtypeStruct(shape, f32) for shape in moved),
-        in_specs=[anywhere] * 4,
-        out_specs=(spec,) * 6,
+        out_shape=tuple(pltpu.VMEM(shape, f32) for shape in moved),
+        in_specs=[far] * 4,
+        out_specs=(spec,) * 7,
         scratch_shapes=[vmem(*velocity.shape), vmem(*density.shape), vmem(*density.shape)]
         + [vmem(4, *fine), vmem(*packed), vmem(CYCLES, *packed), vmem(CYCLES, *fine)]
         + [vmem(*coarse)] * 2
         + [vmem(*fine)] * 7 + [vmem(*density.shape)] + [vmem(*fine)] * 2
         + [vmem(*coarse)] * 6 + [vmem(half, cells_y, cells_z)] + [vmem(*coarse)] * 2
-        + [dma((3,))] + [dma((near,))] * 2 + [dma((wide,))] * 2
+        + [dma((4,))] + [dma((near,))] * 2 + [dma((wide,))] * 2
         + [dma((CYCLES, wide))] * 2 + [dma((CYCLES, near))] * 2 + [dma((side,))] * 2,
-        compiler_params=pltpu.CompilerParams(collective_id=0, has_side_effects=True),
+        compiler_params=pltpu.CompilerParams(
+            collective_id=0, has_side_effects=True, vmem_limit_bytes=16 << 20
+        ),
         name="projection",
-    )(velocity, density, source, species)
+    )(*(pltpu.with_memory_space_constraint(a, pltpu.HBM) for a in (velocity, density, source, species)))
     return pl.pallas_call(
         transport,
         out_shape=tuple(jax.ShapeDtypeStruct(a.shape, f32) for a in (velocity, density, species)),
         in_specs=[spec] * 7,
         out_specs=(spec,) * 3,
+        compiler_params=pltpu.CompilerParams(vmem_limit_bytes=8 << 20),
         name="transport",
-    )(*between, species)
+    )(*between)
 
 
 def solution(mesh):

time: 28.9 us -> 27 us (0.934)
  Pallas kernels: 28.1 us -> 26.2 us
    pallas_call x1, Pallas kernels: 2.17 us -> 1.03 us  [local(): pl.pallas_call(transport, out_shape=tuple((jax.ShapeDtypeStruct(a.shape,...]
    pallas_call x1, Pallas kernels: 25.9 us -> 25.2 us  [local(): pl.pallas_call(functools.partial(kernel, slabs, crosses), out_shape=tuple...]
where the time goes in v1:
time: 27 us; the launch traced here: 26.9 us
  Pallas kernels  26.2 us (97%)
  between operations  0.64 us (2%)
    pallas_call x1, Pallas kernels, local(): pl.pallas_call(functools.partial(kernel, slabs, crosses), out_shape=tuple...  25.2 us
    pallas_call x1, Pallas kernels, local(): pl.pallas_call(transport, out_shape=tuple((jax.ShapeDtypeStruct(a.shape,...  1.03 us

profile of v1, /device:TPU:0, one launch (start us, length us, event | category | flops | bytes accessed | tf_op | source)
XLA Modules:
  0.0 26.9 jit_solution(4179030430577737799)
XLA Ops:
  0.6 25.2 %projection.1 = (f32[6,16,128]{2,1,0:T(8,128)S(1)}, f32[4,32,128]{2,1,0:T(8,128)S(1)}, f32[4,16,128]{2,1,0:T(8,128)S(1)}, f32[4,16,128]{2,1,0:T(8,128)S(1)}, f32...) custom-call(f32[3,4,16,128]{3,2,1,0:T(8,128)} %velocity_in.1, ...), custom_call_target="tpu_custom_call" | custom-call | tf_op jit(solution)/shard_map/projection/pallas_call | solution.py:386
  25.8 1.0 %transport.1 = (f32[3,4,16,128]{3,2,1,0:T(8,128)}, f32[4,16,128]{2,1,0:T(8,128)}, f32[9,4,16,128]{3,2,1,0:T(8,128)}) custom-call(f32[6,16,128]{2,1,0:T(8,128)S(1)} %get-tuple-element.10.in_x, f32[4,32,128]{2,1,0:T(8,128)S(1)} %get-tuple-element.11.in_y, f32[4,16,128]{2,1,0:T(8,128)S(1)} %get-tuple-element.12.in_z, f32[4,16,128]{2,1,0:T(8,128)S(1)} %get-tuple-element.13.in_p, ...), custom_call_target="tpu_custom_call" | custom-call | tf_op jit(solution)/shard_map/transport/pallas_call | solution.py:403

commit v2 on v1

v2 whole, which is shorter than its diff:
```python
import functools

import jax
import jax.numpy as jnp
from jax import lax
from jax.experimental import pallas as pl
from jax.experimental.pallas import tpu as pltpu
from jax.sharding import PartitionSpec as P

CYCLES = 2
COARSE = 4
damping = 0.8
time_step = 0.25
MESH = pl.DeviceIdType.MESH
HX = 5
HY = 8
EVEN, ODD = 0, 1
OWN = 3

EDGES = (-5, -1, 0, 3, 4, 7, 8, 12)
BELOW = {-1: 2, 3: 4, 7: 6, 11: 7}
ABOVE = {-4: 0, 0: 1, 4: 3, 8: 5}


def kernel(
    slabs, crosses, velocity_in, density_in, source_in, species,
    out_x, out_y, out_z, out_p, rim_x, rim_y, kinds,
    velocity, density, source, stage, stage_x, stage_y, stage_c,
    near, later, edge_x, edge_y, press, coarse_m, packed_r, given,
    xa, xb, ya, yb, za, zb, goal, scale_back, pa, pb,
    cxa, cxb, cya, cyb, cza, czb, ca, cb, fold, spread, rim_v, rim_w, in_sem, *sems,
):
    cells_x, cells_y, cells_z = density.shape
    rows = 2 * cells_x
    wx, wy = rows + 2 * HX, cells_y + 2 * HY
    half_y = cells_y // 2
    blocks = packed_r.shape[1]
    own_y = pl.ds(HY, cells_y)
    own_c = pl.ds(half_y, half_y)
    slab, cross = lax.axis_index("slab"), lax.axis_index("cross")
    odd = slab % 2 == 1
    f32 = jnp.float32

    def there(dx, dy):
        return (slab + dx >= 0) & (slab + dx < slabs) & (cross + dy >= 0) & (cross + dy < crosses)

    groups = []

    def exchange(moves):
        at = len(groups)
        send, recv = sems[2 * at], sems[2 * at + 1]
        groups.append(len(moves))

        def copy(index):
            _, dx, dy, src, dst = moves[index]
            return pltpu.make_async_remote_copy(
                src_ref=src, dst_ref=dst, send_sem=send.at[index], recv_sem=recv.at[index],
                device_id=(slab + dx, cross + dy), device_id_type=MESH,
            )

        def each(role, sender, act):
            for index, (by, dx, dy, _, _) in enumerate(moves):
                if sender and by == role:
                    @pl.when(there(dx, dy))
                    def _():
                        act(copy(index))
                if not sender and (by + dx) % 2 == role:
                    @pl.when(there(-dx, -dy))
                    def _():
                        act(copy(index))

        def start(role):
            each(role, True, lambda c: c.start())

        def arrive(role):
            each(role, False, lambda c: c.wait_recv())

        def leave(role):
            each(role, True, lambda c: c.wait_send())

        return start, arrive, leave

    def cut_y(dy, low, high, home=0, rim=HY, span=cells_y):
        depth = high - low + 1
        if dy > 0:
            return pl.ds(home + span - high, depth), pl.ds(rim - high, depth)
        return pl.ds(home + low - 1, depth), pl.ds(rim + span + low - 1, depth)

    whole = slice(None)
    first, rest = [], []
    for by, base, out in ((EVEN, 0, -1), (ODD, cells_x, 2)):
        to = 1 - by
        lo_edge, hi_edge = EDGES.index(base), EDGES.index(base + cells_x - 1)
        at = rows if by == EVEN else -cells_x
        touch = 0 if by == EVEN else cells_x - 1
        edge = EDGES.index(at + touch)

        def seen(deep, count, at=at, by=by):
            start = deep - 1 if by == EVEN else cells_x - deep - count + 1
            return pl.ds(start, count), pl.ds(HX + at + start, count)

        for dy in (-1, 1):
            j, k = (2, 0) if dy > 0 else (1, 3)
            src, dst = seen(1, 2)
            ys, yd = cut_y(dy, 1, 2)
            first.append((by, out, dy, stage.at[whole, src, ys], near.at[whole, dst, yd]))
            ys, yd = cut_y(dy, 1, 4)
            first.append((by, out, dy, stage_x.at[min(touch, 1), ys], edge_x.at[edge, yd]))
            first.append((by, out, dy, stage_y.at[whole, j], edge_y.at[pl.ds(HX + at, cells_x), k]))
        src, dst = seen(1, 3)
        first.append((by, out, 0, stage.at[whole, src], near.at[whole, dst, own_y]))
        first.append((by, out, 0, stage_x.at[min(touch, 1)], edge_x.at[edge, own_y]))
        first.append((by, out, 0, stage_y.at[whole, pl.ds(1, 2)], edge_y.at[pl.ds(HX + at, cells_x), pl.ds(1, 2)]))
        mine = pl.ds(HX + base, cells_x)
        for dy in (-1, 1):
            j, k = (2, 0) if dy > 0 else (1, 3)
            ys, yd = cut_y(dy, 1, 3)
            first.append((by, to, dy, stage.at[whole, whole, ys], near.at[whole, mine, yd]))
            ys, yd = cut_y(dy, 1, 4)
            first.append((by, to, dy, stage_x.at[whole, ys], edge_x.at[pl.ds(lo_edge, 2), yd]))
            first.append((by, to, dy, stage_y.at[whole, j], edge_y.at[mine, k]))
        if by == EVEN:
            first.append((by, 1, 0, stage, near.at[whole, mine, own_y]))
            first.append((by, 1, 0, stage_x, edge_x.at[pl.ds(lo_edge, 2), own_y]))
            first.append((by, 1, 0, stage_y.at[whole, pl.ds(1, 2)], edge_y.at[mine, pl.ds(1, 2)]))
            first.append((by, 1, 0, stage_c, coarse_m.at[OWN, own_c]))

        for dy in (-1, 1):
            for deep, low, high in ((1, 3, 4), (3, 1, 2)):
                src, dst = seen(deep, 2)
                ys, yd = cut_y(dy, low, high)
                rest.append((by, out, dy, stage.at[whole, src, ys], later.at[whole, dst, yd]))
        src, dst = seen(4, 1)
        rest.append((by, out, 0, stage.at[whole, src], later.at[whole, dst, own_y]))
        far, row, lands = (3, cells_x - 1, -HX) if by == EVEN else (-2, 0, rows + HX - 1)
        rest.append((by, far, 0, stage.at[0, row], later.at[0, HX + lands, own_y]))
        rest.append((by, far, 0, stage_x.at[min(row, 1)], edge_x.at[EDGES.index(lands), own_y]))
        for dy in (-1, 1):
            ys, yd = cut_y(dy, 4, 5)
            rest.append((by, to, dy, stage.at[whole, whole, ys], later.at[whole, mine, yd]))

    def coarse_moves(ref):
        moves = []
        for dy in (-1, 1, 0):
            for dx, src, dst, reach in (
                (2, OWN, OWN - 2, 5), (-2, OWN, OWN + 2, 5), (4, OWN + 1, OWN - 3, 1), (-4, OWN, OWN + 4, 1), (0, OWN, OWN, 6),
            ):
                if dx == 0 and dy == 0:
                    continue
                count = 1 if abs(dx) == 4 else 2
                ys, yd = (own_c, own_c) if dy == 0 else cut_y(dy, 1, reach, half_y, half_y, half_y)
                moves.append((ODD, dx, dy, ref.at[pl.ds(src, count), ys], ref.at[pl.ds(dst, count), yd]))
        return moves

    def press_moves(ref, reach):
        moves = []
        low, high = (pl.ds(HX, reach), pl.ds(HX + rows, reach)), (pl.ds(HX + rows - reach, reach), pl.ds(HX - reach, reach))
        corner = reach - 1
        low_c, high_c = (pl.ds(HX, corner), pl.ds(HX + rows, corner)), (pl.ds(HX + rows - corner, corner), pl.ds(HX - corner, corner))
        for dy in (-1, 1):
            ys, yd = cut_y(dy, 1, corner, HY)
            moves.append((ODD, 2, dy, ref.at[high_c[0], ys], ref.at[high_c[1], yd]))
            moves.append((ODD, -2, dy, ref.at[low_c[0], ys], ref.at[low_c[1], yd]))
        moves.append((ODD, 2, 0, ref.at[high[0], own_y], ref.at[high[1], own_y]))
        moves.append((ODD, -2, 0, ref.at[low[0], own_y], ref.at[low[1], own_y]))
        own_x = pl.ds(HX, rows)
        for dy in (-1, 1):
            ys, yd = cut_y(dy, 1, reach, HY)
            moves.append((ODD, 0, dy, ref.at[own_x, ys], ref.at[own_x, yd]))
        return moves

    def species_moves():
        moves = []
        for by in (EVEN, ODD):
            for dx, dy in ((-1, 0), (1, 0), (0, -1), (0, 1)):
                if dx != 0:
                    src, dst = kinds.at[:, cells_x - 1 if dx > 0 else 0], rim_x.at[0 if dx > 0 else 1]
                else:
                    src, dst = kinds.at[:, :, cells_y - 1 if dy > 0 else 0], rim_y.at[0 if dy > 0 else 1]
                moves.append((by, dx, dy, src, dst))
        return moves

    back = [(ODD, -1, 0, pb.at[pl.ds(HX - 1, cells_x + 2)], given)]
    sides = [
        (ODD, -1, 0, rim_v.at[0], out_x.at[0]),
        (ODD, -1, 0, rim_v.at[1], out_x.at[cells_x + 1]),
        (ODD, -1, 0, rim_w.at[whole, 0], out_y.at[whole, HY - 1]),
        (ODD, -1, 0, rim_w.at[whole, 1], out_y.at[whole, HY + cells_y]),
    ]

    f_x, g_x, m_x = exchange(first), exchange(rest), exchange(coarse_moves(coarse_m))
    r_x = [exchange(coarse_moves(packed_r.at[at])) for at in range(CYCLES)]
    p_x = [exchange(press_moves(press.at[at], HX - at)) for at in range(CYCLES)]
    s_x, b_x, v_x = exchange(species_moves()), exchange(back), exchange(sides)
    every = (f_x, g_x, m_x, *r_x, *p_x, s_x, b_x, v_x)

    def grids(count):
        lane = lax.broadcasted_iota(jnp.int32, (count, cells_z), 1)
        row = lax.broadcasted_iota(jnp.int32, (count, cells_z), 0)
        return row, lane

    def next_z(v, k=1):
        return pltpu.roll(v, cells_z - k, 1)

    def prev_z(v, k=1):
        return pltpu.roll(v, k, 1)

    def next_y(v):
        return pltpu.roll(v, v.shape[0] - 1, 0)

    def prev_y(v):
        return pltpu.roll(v, 1, 0)

    def pack(two):
        lane = grids(two[0].shape[0])[1]
        return jnp.where(lane % 2 == 0, two[0] + next_z(two[0]), two[1] + prev_z(two[1]))

    inputs = [
        pltpu.make_async_copy(src, dst, in_sem.at[at])
        for at, (src, dst) in enumerate(
            ((velocity_in, velocity), (density_in, density), (source_in, source), (species, kinds))
        )
    ]
    for copy in inputs:
        copy.start()
    for ref in (near, later, edge_x, edge_y, coarse_m, packed_r, press, rim_x, rim_y):
        ref[...] = jnp.zeros(ref.shape, f32)

    barrier = pltpu.get_barrier_semaphore()
    greet = {ODD: set(), EVEN: set()}
    for moves in (first, rest, coarse_moves(coarse_m), press_moves(press.at[0], HX), species_moves(), back):
        for by, dx, dy, _, _ in moves:
            greet[by].add((dx, dy))
            greet[(by + dx) % 2].add((-dx, -dy))
    count = jnp.int32(0)
    for role in (EVEN, ODD):
        for dx, dy in sorted(greet[role]):
            here = there(dx, dy) & (odd if role == ODD else jnp.logical_not(odd))
            count = count + here.astype(jnp.int32)

            @pl.when(here)
            def _():
                pl.semaphore_signal(barrier, inc=1, device_id=(slab + dx, cross + dy), device_id_type=MESH)

    for copy in inputs[:3]:
        copy.wait()
    row_o, lane_o = grids(cells_y)
    for x in range(cells_x):
        v0, v1, v2 = velocity[0, x], velocity[1, x], velocity[2, x]
        dz = jnp.where(lane_o == cells_z - 1, 0.0, next_z(v2)) - jnp.where(lane_o == 0, 0.0, prev_z(v2))
        dy = jnp.where(row_o == cells_y - 1, 0.0, next_y(v1)) - jnp.where(row_o == 0, 0.0, prev_y(v1))
        t = dy + dz
        if x + 1 < cells_x:
            t = t + velocity[0, x + 1]
        if x > 0:
            t = t - velocity[0, x - 1]
        m = 1.0 / density[x]
        stage[0, x] = m
        stage[1, x] = 0.5 * t - source[x]
        fold[x] = m
        stage_y[x, pl.ds(1, 1)] = 0.5 * v1[0:1]
        stage_y[x, pl.ds(2, 1)] = 0.5 * v1[cells_y - 1 : cells_y]
        if x == 0:
            stage_x[0] = 0.5 * v0
        if x == cells_x - 1:
            stage_x[1] = 0.5 * v0

    def folded(x):
        return fold[x, pl.ds(0, half_y, stride=2)] + fold[x, pl.ds(1, half_y, stride=2)]

    mean = 0.125 * pack([folded(0) + folded(1), folded(2) + folded(3)])
    stage_c[...] = mean
    pl.semaphore_wait(barrier, count)

    @pl.when(jnp.logical_not(odd))
    def _():
        f_x[0](EVEN)
        g_x[0](EVEN)
        inputs[3].wait()
        s_x[0](EVEN)
        b_x[1](EVEN)
        for x in range(cells_x):
            m = stage[0, x]
            p = given[1 + x, own_y]
            out_x[1 + x] = velocity[0, x] - m * (0.5 * (given[2 + x, own_y] - given[x, own_y]))
            grad = given[1 + x, pl.ds(HY + 1, cells_y)] - given[1 + x, pl.ds(HY - 1, cells_y)]
            out_y[x, own_y] = velocity[1, x] - m * (0.5 * grad)
            row_o, lane_o = grids(cells_y)
            dz = jnp.where(lane_o == cells_z - 1, 0.0, next_z(p)) - jnp.where(lane_o == 0, 0.0, prev_z(p))
            out_z[x] = velocity[2, x] - m * (0.5 * dz)
            out_p[x] = p
        v_x[1](EVEN)
        s_x[1](EVEN)
        for x in every:
            x[2](EVEN)

    @pl.when(odd)
    def _():
        f_x[0](ODD)
        g_x[0](ODD)
        row_w, lane_w = grids(wy)
        row_c, lane_c = grids(2 * half_y + half_y)
        even_c = lane_c % 2 == 0
        row_o, lane_o = grids(cells_y)
        mine = pl.ds(HX + cells_x, cells_x)
        near[0, mine, own_y] = stage[0]
        near[1, mine, own_y] = stage[1]
        edge_x[pl.ds(EDGES.index(cells_x), 2), own_y] = stage_x[...]
        edge_y[mine, pl.ds(1, 2)] = stage_y[:, pl.ds(1, 2)]
        coarse_m[OWN + 1, own_c] = stage_c[...]
        f_x[1](ODD)
        m_x[0](ODD)

        def fine_setup(span, full):
            def mob(x):
                return near[0, x] + later[0, x] if full else near[0, x]

            for x in span:
                m = mob(x)
                lo_x, hi_x = m + mob(x - 1), m + mob(x + 1)
                lo_y, hi_y = m + prev_y(m), m + next_y(m)
                lo_z = m + jnp.where(lane_w == 0, 0.0, prev_z(m))
                hi_z = m + jnp.where(lane_w == cells_z - 1, 0.0, next_z(m))
                diag = (lo_x + hi_x) + (lo_y + hi_y) + (lo_z + hi_z)
                inside = m > 0.0
                inv = jnp.where(inside, damping / jnp.where(inside, diag, 1.0), 0.0)
                xa[x], xb[x] = lo_x * inv, hi_x * inv
                ya[x], yb[x] = lo_y * inv, hi_y * inv
                za[x] = jnp.where(lane_w == 0, 0.0, lo_z * inv)
                zb[x] = jnp.where(lane_w == cells_z - 1, 0.0, hi_z * inv)
                t = near[1, x] + later[1, x] if full else near[1, x]
                at = x - HX
                if at in BELOW and (full or BELOW[at] not in (0, 7)):
                    t = t + edge_x[BELOW[at]]
                if at in ABOVE and (full or ABOVE[at] not in (0, 7)):
                    t = t - edge_x[ABOVE[at]]

                def side(j):
                    return jnp.broadcast_to(edge_y[x, pl.ds(j, 1)], t.shape)

                t = t + jnp.where(row_w == HY - 1, side(1), 0.0) - jnp.where(row_w == HY, side(0), 0.0)
                t = t + jnp.where(row_w == HY + cells_y - 1, side(3), 0.0)
                t = t - jnp.where(row_w == HY + cells_y, side(2), 0.0)
                b = t * (inv + inv)
                goal[x] = b
                if not full:
                    pa[x] = -b
                    if HX <= x < HX + rows:
                        scale_back[x - HX] = (diag * (0.5 / damping))[HY : HY + cells_y]

        fine_setup(range(HX - 2, HX + rows + 2), False)

        def sweep(src, dst, low, high):
            for x in range(low, high):
                v = src[x]
                t = xa[x] * src[x - 1] + xb[x] * src[x + 1]
                t = t + (ya[x] * prev_y(v) + yb[x] * next_y(v))
                t = t + (za[x] * prev_z(v) + zb[x] * next_z(v))
                dst[x] = (1.0 - damping) * v + (t - goal[x])

        def beside(ref, low, high):
            up = {b: next_z(ref[b]) for b in range(max(low - 1, 0), high)}
            down = {b: prev_z(ref[b]) for b in range(low, min(high + 1, blocks))}
            for b in range(low, high):
                yield b, jnp.where(even_c, up[max(b - 1, 0)], down[b]), jnp.where(even_c, up[b], down[min(b + 1, blocks - 1)])

        def coarse_setup():
            for b, lo, hi in beside(coarse_m, 0, blocks):
                m = coarse_m[b]
                if b == 0:
                    lo = jnp.where(even_c, 0.0, lo)
                if b == blocks - 1:
                    hi = jnp.where(even_c, hi, 0.0)
                lo_x, hi_x = m + lo, m + hi
                lo_y, hi_y = m + prev_y(m), m + next_y(m)
                lo_z = m + jnp.where(lane_c < 2, 0.0, prev_z(m, 2))
                hi_z = m + jnp.where(lane_c >= cells_z - 2, 0.0, next_z(m, 2))
                diag = (lo_x + hi_x) + (lo_y + hi_y) + (lo_z + hi_z)
                inside = m > 0.0
                inv = jnp.where(inside, damping / jnp.where(inside, diag, 1.0), 0.0)
                cxa[b], cxb[b] = lo_x * inv, hi_x * inv
                cya[b], cyb[b] = lo_y * inv, hi_y * inv
                cza[b] = jnp.where(lane_c < 2, 0.0, lo_z * inv)
                czb[b] = jnp.where(lane_c >= cells_z - 2, 0.0, hi_z * inv)

        def own_inverse(b):
            m = coarse_m[b]
            lo = jnp.where(even_c, next_z(coarse_m[b - 1]), prev_z(m))
            hi = jnp.where(even_c, next_z(m), prev_z(coarse_m[b + 1]))
            total = (lo + hi) + (prev_y(m) + next_y(m)) + 6.0 * m
            total = total + jnp.where(lane_c < 2, 0.0, prev_z(m, 2)) + jnp.where(lane_c >= cells_z - 2, 0.0, next_z(m, 2))
            return damping / total[half_y : 2 * half_y]

        def coarse_sweep(src, dst, right, low, high):
            for b, lo, hi in beside(src, low, high):
                v = src[b]
                t = cxa[b] * lo + cxb[b] * hi
                t = t + (cya[b] * prev_y(v) + cyb[b] * next_y(v))
                t = t + (cza[b] * prev_z(v, 2) + czb[b] * next_z(v, 2))
                dst[b] = (1.0 - damping) * v + (t - right[b])

        def correct(at, pre, free, reach):
            press[at, pl.ds(HX, rows), own_y] = pre[pl.ds(HX, rows), own_y]
            for x in range(HX, HX + rows, 2):
                total = None
                for w in (x, x + 1):
                    v = pre[w]
                    t = xa[w] * pre[w - 1] + xb[w] * pre[w + 1]
                    t = t + (ya[w] * prev_y(v) + yb[w] * next_y(v))
                    t = t + (za[w] * prev_z(v) + zb[w] * next_z(v))
                    d = (damping * v - (t - goal[w]))[HY : HY + cells_y] * scale_back[w - HX]
                    total = d if total is None else total + d
                fold[(x - HX) // 2] = total
            if at == 0:
                m_x[1](ODD)
            for b in range(2):
                packed_r[at, OWN + b, own_c] = pack([folded(2 * b), folded(2 * b + 1)]) * own_inverse(OWN + b)
            r_x[at][0](ODD)
            p_x[at][0](ODD)
            if at == 0:
                coarse_setup()
                inputs[3].wait()
                s_x[0](ODD)
                g_x[1](ODD)
                fine_setup(range(1, wx - 1), True)
            r_x[at][1](ODD)
            right = packed_r.at[at]
            for b in range(blocks):
                ca[b] = -right[b]
            coarse_sweep(ca, cb, right, 0, blocks)
            coarse_sweep(cb, ca, right, 1, blocks - 1)
            coarse_sweep(ca, cb, right, 1, blocks - 1)
            margin = half_y - HY // 2
            for q in range(-3, rows // 2 + 3):
                v = cb[OWN + q // 2]
                v = jnp.where(even_c, v, prev_z(v)) if q % 2 == 0 else jnp.where(even_c, next_z(v), v)
                v = v[margin : margin + wy // 2]
                spread[q + 3, pl.ds(0, wy // 2, stride=2)] = v
                spread[q + 3, pl.ds(1, wy // 2, stride=2)] = v
            p_x[at][1](ODD)
            low, high = HX - reach - 2, HX + rows + reach + 2
            for x in range(low, high):
                pre[x] = press[at, x] + spread[(x - HX) // 2 + 3]
            sweep(pre, free, low + 1, high - 1)
            sweep(free, pre, low + 2, high - 2)

        sweep(pa, pb, HX - 1, HX + rows + 1)
        correct(0, pb, pa, 3)
        sweep(pb, pa, HX - 2, HX + rows + 2)
        sweep(pa, pb, HX - 1, HX + rows + 1)
        correct(1, pb, pa, 2)
        last = pb
        b_x[0](ODD)

        def along_x(x):
            return near[0, x, own_y] * (0.5 * (last[x + 1, own_y] - last[x - 1, own_y]))

        def along_y(x, y):
            one = pl.ds(y, 1)
            return near[0, x, one] * (0.5 * (last[x, pl.ds(y + 1, 1)] - last[x, pl.ds(y - 1, 1)]))

        def edge(at):
            v = edge_x[EDGES.index(at), own_y]
            return (v + v) - along_x(HX + at)

        def ends(x):
            lo, hi = edge_y[x, pl.ds(0, 1)], edge_y[x, pl.ds(3, 1)]
            return (lo + lo) - along_y(x, HY - 1), (hi + hi) - along_y(x, HY + cells_y)

        rim_v[0] = edge(-1)
        rim_v[1] = edge(cells_x)
        for x in range(cells_x):
            lo, hi = ends(HX + x)
            rim_w[x, pl.ds(0, 1)] = lo
            rim_w[x, pl.ds(1, 1)] = hi
        v_x[0](ODD)
        out_x[0] = edge(cells_x - 1)
        out_x[cells_x + 1] = edge(rows)
        for x in range(cells_x):
            w = HX + cells_x + x
            m = near[0, w, own_y]
            p = last[w, own_y]
            out_x[1 + x] = velocity[0, x] - along_x(w)
            grad = last[w, pl.ds(HY + 1, cells_y)] - last[w, pl.ds(HY - 1, cells_y)]
            out_y[x, own_y] = velocity[1, x] - m * (0.5 * grad)
            lo, hi = ends(w)
            out_y[x, pl.ds(HY - 1, 1)] = lo
            out_y[x, pl.ds(HY + cells_y, 1)] = hi
            dz = jnp.where(lane_o == cells_z - 1, 0.0, next_z(p)) - jnp.where(lane_o == 0, 0.0, prev_z(p))
            out_z[x] = velocity[2, x] - m * (0.5 * dz)
            out_p[x] = p
        s_x[1](ODD)
        for x in every:
            x[2](ODD)

    assert groups == MOVES, groups


MOVES = [34, 18, 14, 14, 14, 8, 8, 8, 1, 4]


def transport(in_x, in_y, in_z, in_p, rim_x, rim_y, species, vel_out, pres_out, spec_out):
    cells_x, cells_y, cells_z = in_p.shape
    lane_o = lax.broadcasted_iota(jnp.int32, (cells_y, cells_z), 1)
    row_o = lax.broadcasted_iota(jnp.int32, (cells_y, cells_z), 0)

    def next_z(v):
        return pltpu.roll(v, cells_z - 1, 1)

    def prev_z(v):
        return pltpu.roll(v, 1, 1)

    def next_y(v):
        return pltpu.roll(v, v.shape[0] - 1, 0)

    def prev_y(v):
        return pltpu.roll(v, 1, 0)

    mid = slice(HY, HY + cells_y)
    pres_out[...] = in_p[...]
    move_x = [in_x[x] for x in range(cells_x + 2)]
    for x in range(cells_x):
        move_y, move_z = in_y[x], in_z[x]
        vel_out[0, x] = move_x[x + 1]
        vel_out[1, x] = move_y[mid]
        vel_out[2, x] = move_z
        lo_x, hi_x = 0.5 * (move_x[x] + move_x[x + 1]), 0.5 * (move_x[x + 1] + move_x[x + 2])
        lo_y, hi_y = (0.5 * (move_y + prev_y(move_y)))[mid], (0.5 * (move_y + next_y(move_y)))[mid]
        lo_z = 0.5 * (move_z + jnp.where(lane_o == 0, 0.0, prev_z(move_z)))
        hi_z = 0.5 * (move_z + jnp.where(lane_o == cells_z - 1, 0.0, next_z(move_z)))

        def into(flow):
            return time_step * jnp.maximum(flow, 0.0)

        def back(flow):
            return -time_step * jnp.minimum(flow, 0.0)

        keep = 1.0 - (into(hi_x) + into(hi_y) + into(hi_z)) - (back(lo_x) + back(lo_y) + back(lo_z))
        from_xl, from_xu = into(lo_x), back(hi_x)
        from_yl, from_yu = into(lo_y), back(hi_y)
        from_zl = jnp.where(lane_o == 0, 0.0, into(lo_z))
        from_zu = jnp.where(lane_o == cells_z - 1, 0.0, back(hi_z))
        for s in range(species.shape[0]):
            q = species[s, x]
            xl = rim_x[0, s] if x == 0 else species[s, x - 1]
            xu = rim_x[1, s] if x == cells_x - 1 else species[s, x + 1]
            yl = jnp.where(row_o == 0, rim_y[0, s, pl.ds(x, 1)], prev_y(q))
            yu = jnp.where(row_o == cells_y - 1, rim_y[1, s, pl.ds(x, 1)], next_y(q))
            total = keep * q + (from_xl * xl + from_xu * xu) + (from_yl * yl + from_yu * yu)
            spec_out[s, x] = total + (from_zl * prev_z(q) + from_zu * next_z(q))


def local(slabs, crosses, velocity, density, source, species):
    cells_x, cells_y, cells_z = density.shape
    assert cells_x == 4 and cells_y == 2 * HY and slabs % 2 == 0
    rows = 2 * cells_x
    wx, wy = rows + 2 * HX, cells_y + 2 * HY
    half_y = cells_y // 2
    kinds = species.shape[0]
    f32 = jnp.float32

    def vmem(*shape):
        return pltpu.VMEM(shape, f32)

    blocks = 2 * OWN + 2
    fine, coarse = (wx, wy, cells_z), (blocks, 3 * half_y, cells_z)
    dma = pltpu.SemaphoreType.DMA
    spec = pl.BlockSpec(memory_space=pltpu.VMEM)
    far = pl.BlockSpec(memory_space=pltpu.HBM)
    moved = [
        (cells_x + 2, cells_y, cells_z), (cells_x, wy, cells_z), density.shape, density.shape,
        (2, kinds, cells_y, cells_z), (2, kinds, cells_x, cells_z), species.shape,
    ]
    between = pl.pallas_call(
        functools.partial(kernel, slabs, crosses),
        out_shape=tuple(pltpu.VMEM(shape, f32) for shape in moved),
        in_specs=[far] * 4,
        out_specs=(spec,) * 7,
        scratch_shapes=[vmem(*velocity.shape), vmem(*density.shape), vmem(*density.shape)]
        + [vmem(2, *density.shape), vmem(2, cells_y, cells_z), vmem(cells_x, 8, cells_z), vmem(half_y, cells_z)]
        + [vmem(2, *fine)] * 2 + [vmem(len(EDGES), wy, cells_z), vmem(wx, 8, cells_z)]
        + [vmem(CYCLES, *fine), vmem(*coarse), vmem(CYCLES, *coarse), vmem(cells_x + 2, wy, cells_z)]
        + [vmem(*fine)] * 7 + [vmem(rows, cells_y, cells_z)] + [vmem(*fine)] * 2
        + [vmem(*coarse)] * 8 + [vmem(cells_x, cells_y, cells_z), vmem(rows // 2 + 6, wy, cells_z)]
        + [vmem(2, cells_y, cells_z), vmem(cells_x, 8, cells_z)]
        + [dma((4,))] + [dma((n,)) for n in MOVES for _ in range(2)],
        compiler_params=pltpu.CompilerParams(
            collective_id=0, has_side_effects=True, vmem_limit_bytes=16 << 20
        ),
        name="projection",
    )(*(pltpu.with_memory_space_constraint(a, pltpu.HBM) for a in (velocity, density, source, species)))
    return pl.pallas_call(
        transport,
        out_shape=tuple(jax.ShapeDtypeStruct(a.shape, f32) for a in (velocity, density, species)),
        in_specs=[spec] * 7,
        out_specs=(spec,) * 3,
        compiler_params=pltpu.CompilerParams(vmem_limit_bytes=8 << 20),
        name="transport",
    )(*between)


def solution(mesh):
    plane, stack = P("slab", "cross", None), P(None, "slab", "cross", None)
    return jax.shard_map(
        functools.partial(local, mesh.shape["slab"], mesh.shape["cross"]),
        mesh=mesh,
        in_specs=(stack, plane, plane, stack),
        out_specs=(stack, plane, stack),
        check_vma=False,
    )
```

time: 27 us -> 25.4 us (0.941)
  Pallas kernels: 26.2 us -> 24.6 us
    pallas_call x1, Pallas kernels: 25.2 us -> 23.5 us  [local(): pl.pallas_call(functools.partial(kernel, slabs, crosses), out_shape=tuple...]
where the time goes in v2:
time: 25.4 us; the launch traced here: 25.2 us
  Pallas kernels  24.6 us (97%)
  between operations  0.64 us (3%)
    pallas_call x1, Pallas kernels, local(): pl.pallas_call(functools.partial(kernel, slabs, crosses), out_shape=tuple...  23.5 us
    pallas_call x1, Pallas kernels, local(): pl.pallas_call(transport, out_shape=tuple((jax.ShapeDtypeStruct(a.shape,...  1.03 us

profile of v2, /device:TPU:0, one launch (start us, length us, event | category | flops | bytes accessed | tf_op | source)
XLA Modules:
  0.0 25.2 jit_solution(2965487599096496277)
XLA Ops:
  0.6 23.5 %projection.1 = (f32[6,16,128]{2,1,0:T(8,128)S(1)}, f32[4,32,128]{2,1,0:T(8,128)S(1)}, f32[4,16,128]{2,1,0:T(8,128)S(1)}, f32[4,16,128]{2,1,0:T(8,128)S(1)}, f32...) custom-call(f32[3,4,16,128]{3,2,1,0:T(8,128)} %velocity_in.1, ...), custom_call_target="tpu_custom_call" | custom-call | tf_op jit(solution)/shard_map/projection/pallas_call | solution.py:574
  24.2 1.0 %transport.1 = (f32[3,4,16,128]{3,2,1,0:T(8,128)}, f32[4,16,128]{2,1,0:T(8,128)}, f32[9,4,16,128]{3,2,1,0:T(8,128)}) custom-call(f32[6,16,128]{2,1,0:T(8,128)S(1)} %get-tuple-element.10.in_x, f32[4,32,128]{2,1,0:T(8,128)S(1)} %get-tuple-element.11.in_y, f32[4,16,128]{2,1,0:T(8,128)S(1)} %get-tuple-element.12.in_z, f32[4,16,128]{2,1,0:T(8,128)S(1)} %get-tuple-element.13.in_p, ...), custom_call_target="tpu_custom_call" | custom-call | tf_op jit(solution)/shard_map/transport/pallas_call | solution.py:592

commit v3 on v2

--- a/solution.py
+++ b/solution.py
@@ -28,7 +28,7 @@
     velocity, density, source, stage, stage_x, stage_y, stage_c,
     near, later, edge_x, edge_y, press, coarse_m, packed_r, given,
     xa, xb, ya, yb, za, zb, goal, scale_back, pa, pb,
-    cxa, cxb, cya, cyb, cza, czb, ca, cb, fold, spread, rim_v, rim_w, in_sem, *sems,
+    cxa, cxb, cya, cyb, cza, czb, cinv, right, ca, cb, fold, spread, rim_v, rim_w, in_sem, *sems,
 ):
     cells_x, cells_y, cells_z = density.shape
     rows = 2 * cells_x
@@ -141,13 +141,14 @@
 
     def coarse_moves(ref):
         moves = []
-        for dy in (-1, 1, 0):
-            for dx, src, dst, reach in (
-                (2, OWN, OWN - 2, 5), (-2, OWN, OWN + 2, 5), (4, OWN + 1, OWN - 3, 1), (-4, OWN, OWN + 4, 1), (0, OWN, OWN, 6),
-            ):
-                if dx == 0 and dy == 0:
-                    continue
-                count = 1 if abs(dx) == 4 else 2
+        ahead, behind, ahead_far, behind_far, aside = (
+            (2, OWN, OWN - 2, 2, 5), (-2, OWN, OWN + 2, 2, 5), (4, OWN + 1, OWN - 3, 1, 1), (-4, OWN, OWN + 4, 1, 1), (0, OWN, OWN, 2, 6),
+        )
+        for dy, kinds_of in (
+            (-1, (ahead, behind)), (1, (ahead, behind)), (0, (ahead, behind)),
+            (-1, (ahead_far, behind_far)), (1, (ahead_far, behind_far)), (0, (ahead_far, behind_far)), (-1, (aside,)), (1, (aside,)),
+        ):
+            for dx, src, dst, count, reach in kinds_of:
                 ys, yd = (own_c, own_c) if dy == 0 else cut_y(dy, 1, reach, half_y, half_y, half_y)
                 moves.append((ODD, dx, dy, ref.at[pl.ds(src, count), ys], ref.at[pl.ds(dst, count), yd]))
         return moves
@@ -223,24 +224,36 @@
     ]
     for copy in inputs:
         copy.start()
-    for ref in (near, later, edge_x, edge_y, coarse_m, packed_r, press, rim_x, rim_y):
-        ref[...] = jnp.zeros(ref.shape, f32)
-
     barrier = pltpu.get_barrier_semaphore()
     greet = {ODD: set(), EVEN: set()}
-    for moves in (first, rest, coarse_moves(coarse_m), press_moves(press.at[0], HX), species_moves(), back):
+    for moves in (first, rest, species_moves(), back):
         for by, dx, dy, _, _ in moves:
             greet[by].add((dx, dy))
             greet[(by + dx) % 2].add((-dx, -dy))
-    count = jnp.int32(0)
-    for role in (EVEN, ODD):
-        for dx, dy in sorted(greet[role]):
-            here = there(dx, dy) & (odd if role == ODD else jnp.logical_not(odd))
-            count = count + here.astype(jnp.int32)
-
-            @pl.when(here)
+
+    def enter(role):
+        for dx, dy in sorted(greet[role], key=lambda d: (-abs(d[0]) - 2 * abs(d[1]), d)):
+            @pl.when(there(dx, dy))
             def _():
                 pl.semaphore_signal(barrier, inc=1, device_id=(slab + dx, cross + dy), device_id_type=MESH)
+
+    def entered(role):
+        count = jnp.int32(0)
+        for dx, dy in sorted(greet[role]):
+            count = count + there(dx, dy).astype(jnp.int32)
+        return count
+
+    @pl.when(jnp.logical_not(odd))
+    def _():
+        for ref in (rim_x, rim_y):
+            ref[...] = jnp.zeros(ref.shape, f32)
+        enter(EVEN)
+
+    @pl.when(odd)
+    def _():
+        for ref in (near, later, edge_x, edge_y, coarse_m, packed_r, press, rim_x, rim_y):
+            ref[...] = jnp.zeros(ref.shape, f32)
+        enter(ODD)
 
     for copy in inputs[:3]:
         copy.wait()
@@ -270,7 +283,7 @@
 
     mean = 0.125 * pack([folded(0) + folded(1), folded(2) + folded(3)])
     stage_c[...] = mean
-    pl.semaphore_wait(barrier, count)
+    pl.semaphore_wait(barrier, jnp.where(odd, entered(ODD), entered(EVEN)))
 
     @pl.when(jnp.logical_not(odd))
     def _():
@@ -382,16 +395,9 @@
                 cya[b], cyb[b] = lo_y * inv, hi_y * inv
                 cza[b] = jnp.where(lane_c < 2, 0.0, lo_z * inv)
                 czb[b] = jnp.where(lane_c >= cells_z - 2, 0.0, hi_z * inv)
-
-        def own_inverse(b):
-            m = coarse_m[b]
-            lo = jnp.where(even_c, next_z(coarse_m[b - 1]), prev_z(m))
-            hi = jnp.where(even_c, next_z(m), prev_z(coarse_m[b + 1]))
-            total = (lo + hi) + (prev_y(m) + next_y(m)) + 6.0 * m
-            total = total + jnp.where(lane_c < 2, 0.0, prev_z(m, 2)) + jnp.where(lane_c >= cells_z - 2, 0.0, next_z(m, 2))
-            return damping / total[half_y : 2 * half_y]
-
-        def coarse_sweep(src, dst, right, low, high):
+                cinv[b] = inv
+
+        def coarse_sweep(src, dst, low, high):
             for b, lo, hi in beside(src, low, high):
                 v = src[b]
                 t = cxa[b] * lo + cxb[b] * hi
@@ -411,25 +417,25 @@
                     d = (damping * v - (t - goal[w]))[HY : HY + cells_y] * scale_back[w - HX]
                     total = d if total is None else total + d
                 fold[(x - HX) // 2] = total
-            if at == 0:
-                m_x[1](ODD)
             for b in range(2):
-                packed_r[at, OWN + b, own_c] = pack([folded(2 * b), folded(2 * b + 1)]) * own_inverse(OWN + b)
+                packed_r[at, OWN + b, own_c] = pack([folded(2 * b), folded(2 * b + 1)])
             r_x[at][0](ODD)
             p_x[at][0](ODD)
             if at == 0:
-                coarse_setup()
                 inputs[3].wait()
                 s_x[0](ODD)
                 g_x[1](ODD)
                 fine_setup(range(1, wx - 1), True)
+                m_x[1](ODD)
+                coarse_setup()
             r_x[at][1](ODD)
-            right = packed_r.at[at]
             for b in range(blocks):
-                ca[b] = -right[b]
-            coarse_sweep(ca, cb, right, 0, blocks)
-            coarse_sweep(cb, ca, right, 1, blocks - 1)
-            coarse_sweep(ca, cb, right, 1, blocks - 1)
+                r = packed_r[at, b] * cinv[b]
+                right[b] = r
+                ca[b] = -r
+            coarse_sweep(ca, cb, 0, blocks)
+            coarse_sweep(cb, ca, 1, blocks - 1)
+            coarse_sweep(ca, cb, 1, blocks - 1)
             margin = half_y - HY // 2
             for q in range(-3, rows // 2 + 3):
                 v = cb[OWN + q // 2]
@@ -581,7 +587,7 @@
         + [vmem(2, *fine)] * 2 + [vmem(len(EDGES), wy, cells_z), vmem(wx, 8, cells_z)]
         + [vmem(CYCLES, *fine), vmem(*coarse), vmem(CYCLES, *coarse), vmem(cells_x + 2, wy, cells_z)]
         + [vmem(*fine)] * 7 + [vmem(rows, cells_y, cells_z)] + [vmem(*fine)] * 2
-        + [vmem(*coarse)] * 8 + [vmem(cells_x, cells_y, cells_z), vmem(rows // 2 + 6, wy, cells_z)]
+        + [vmem(*coarse)] * 10 + [vmem(cells_x, cells_y, cells_z), vmem(rows // 2 + 6, wy, cells_z)]
         + [vmem(2, cells_y, cells_z), vmem(cells_x, 8, cells_z)]
         + [dma((4,))] + [dma((n,)) for n in MOVES for _ in range(2)],
         compiler_params=pltpu.CompilerParams(

time: 25.4 us -> 22.7 us (0.89)
  Pallas kernels: 24.6 us -> 21.9 us
    pallas_call x1, Pallas kernels: 23.5 us -> 20.9 us  [local(): pl.pallas_call(functools.partial(kernel, slabs, crosses), out_shape=tuple...]
where the time goes in v3:
time: 22.7 us; the launch traced here: 22.5 us
  Pallas kernels  21.9 us (96%)
  between operations  0.64 us (3%)
    pallas_call x1, Pallas kernels, local(): pl.pallas_call(functools.partial(kernel, slabs, crosses), out_shape=tuple...  20.9 us
    pallas_call x1, Pallas kernels, local(): pl.pallas_call(transport, out_shape=tuple((jax.ShapeDtypeStruct(a.shape,...  1.03 us

profile of v3, /device:TPU:0, one launch (start us, length us, event | category | flops | bytes accessed | tf_op | source)
XLA Modules:
  0.0 22.5 jit_solution(2488196477365155503)
XLA Ops:
  0.6 20.9 %projection.1 = (f32[6,16,128]{2,1,0:T(8,128)S(1)}, f32[4,32,128]{2,1,0:T(8,128)S(1)}, f32[4,16,128]{2,1,0:T(8,128)S(1)}, f32[4,16,128]{2,1,0:T(8,128)S(1)}, f32...) custom-call(f32[3,4,16,128]{3,2,1,0:T(8,128)} %velocity_in.1, ...), custom_call_target="tpu_custom_call" | custom-call | tf_op jit(solution)/shard_map/projection/pallas_call | solution.py:580
  21.5 1.0 %transport.1 = (f32[3,4,16,128]{3,2,1,0:T(8,128)}, f32[4,16,128]{2,1,0:T(8,128)}, f32[9,4,16,128]{3,2,1,0:T(8,128)}) custom-call(f32[6,16,128]{2,1,0:T(8,128)S(1)} %get-tuple-element.10.in_x, f32[4,32,128]{2,1,0:T(8,128)S(1)} %get-tuple-element.11.in_y, f32[4,16,128]{2,1,0:T(8,128)S(1)} %get-tuple-element.12.in_z, f32[4,16,128]{2,1,0:T(8,128)S(1)} %get-tuple-element.13.in_p, ...), custom_call_target="tpu_custom_call" | custom-call | tf_op jit(solution)/shard_map/transport/pallas_call | solution.py:598

commit v4 on v3

--- a/solution.py
+++ b/solution.py
@@ -13,7 +13,7 @@
 time_step = 0.25
 MESH = pl.DeviceIdType.MESH
 HX = 5
-HY = 8
+HY = 4
 EVEN, ODD = 0, 1
 OWN = 3
 
@@ -26,7 +26,7 @@
     slabs, crosses, velocity_in, density_in, source_in, species,
     out_x, out_y, out_z, out_p, rim_x, rim_y, kinds,
     velocity, density, source, stage, stage_x, stage_y, stage_c,
-    near, later, edge_x, edge_y, press, coarse_m, packed_r, given,
+    near, later, fifth_m, edge_x, edge_y, press, fifth_p, coarse_m, packed_r, given,
     xa, xb, ya, yb, za, zb, goal, scale_back, pa, pb,
     cxa, cxb, cya, cyb, cza, czb, cinv, right, ca, cb, fold, spread, rim_v, rim_w, in_sem, *sems,
 ):
@@ -35,7 +35,7 @@
     wx, wy = rows + 2 * HX, cells_y + 2 * HY
     half_y = cells_y // 2
     blocks = packed_r.shape[1]
-    own_y = pl.ds(HY, cells_y)
+    own_y = pl.ds(0, cells_y)
     own_c = pl.ds(half_y, half_y)
     slab, cross = lax.axis_index("slab"), lax.axis_index("cross")
     odd = slab % 2 == 1
@@ -58,8 +58,10 @@
                 device_id=(slab + dx, cross + dy), device_id_type=MESH,
             )
 
-        def each(role, sender, act):
+        def each(role, sender, act, only=None):
             for index, (by, dx, dy, _, _) in enumerate(moves):
+                if only is not None and ((dx, dy) == (1, 0)) != only:
+                    continue
                 if sender and by == role:
                     @pl.when(there(dx, dy))
                     def _():
@@ -72,19 +74,22 @@
         def start(role):
             each(role, True, lambda c: c.start())
 
-        def arrive(role):
-            each(role, False, lambda c: c.wait_recv())
+        def arrive(role, only=None):
+            each(role, False, lambda c: c.wait_recv(), only)
 
         def leave(role):
             each(role, True, lambda c: c.wait_send())
 
         return start, arrive, leave
 
-    def cut_y(dy, low, high, home=0, rim=HY, span=cells_y):
+    def cut_y(dy, low, high, home=0, span=cells_y, rim=wy, behind=cells_y):
         depth = high - low + 1
         if dy > 0:
             return pl.ds(home + span - high, depth), pl.ds(rim - high, depth)
-        return pl.ds(home + low - 1, depth), pl.ds(rim + span + low - 1, depth)
+        return pl.ds(home + low - 1, depth), pl.ds(behind + low - 1, depth)
+
+    def fifth(dy):
+        return (cells_y - 5, 3) if dy > 0 else (4, 4)
 
     whole = slice(None)
     first, rest = [], []
@@ -123,7 +128,7 @@
             first.append((by, 1, 0, stage, near.at[whole, mine, own_y]))
             first.append((by, 1, 0, stage_x, edge_x.at[pl.ds(lo_edge, 2), own_y]))
             first.append((by, 1, 0, stage_y.at[whole, pl.ds(1, 2)], edge_y.at[mine, pl.ds(1, 2)]))
-            first.append((by, 1, 0, stage_c, coarse_m.at[OWN, own_c]))
+            first.append((by, 1, 0, stage_c, coarse_m.at[OWN + 1, own_c]))
 
         for dy in (-1, 1):
             for deep, low, high in ((1, 3, 4), (3, 1, 2)):
@@ -136,20 +141,22 @@
         rest.append((by, far, 0, stage.at[0, row], later.at[0, HX + lands, own_y]))
         rest.append((by, far, 0, stage_x.at[min(row, 1)], edge_x.at[EDGES.index(lands), own_y]))
         for dy in (-1, 1):
-            ys, yd = cut_y(dy, 4, 5)
+            ys, yd = cut_y(dy, 4, 4)
             rest.append((by, to, dy, stage.at[whole, whole, ys], later.at[whole, mine, yd]))
-
-    def coarse_moves(ref):
+            y, j = fifth(dy)
+            rest.append((by, to, dy, stage.at[0, whole, y], fifth_m.at[pl.ds(base, cells_x), j]))
+
+    def coarse_moves(ref, own, reach):
         moves = []
-        ahead, behind, ahead_far, behind_far, aside = (
-            (2, OWN, OWN - 2, 2, 5), (-2, OWN, OWN + 2, 2, 5), (4, OWN + 1, OWN - 3, 1, 1), (-4, OWN, OWN + 4, 1, 1), (0, OWN, OWN, 2, 6),
-        )
+        ahead, behind, aside = (2, own, own - 2, 2, reach - 1), (-2, own, own + 2, 2, reach - 1), (0, own, own, 2, reach)
+        count = (reach - 3) // 2
+        ahead_far, behind_far = (4, own + 2 - count, own - 2 - count, count, reach - 5), (-4, own, own + 4, count, reach - 5)
         for dy, kinds_of in (
             (-1, (ahead, behind)), (1, (ahead, behind)), (0, (ahead, behind)),
             (-1, (ahead_far, behind_far)), (1, (ahead_far, behind_far)), (0, (ahead_far, behind_far)), (-1, (aside,)), (1, (aside,)),
         ):
-            for dx, src, dst, count, reach in kinds_of:
-                ys, yd = (own_c, own_c) if dy == 0 else cut_y(dy, 1, reach, half_y, half_y, half_y)
+            for dx, src, dst, count, deep in kinds_of:
+                ys, yd = (own_c, own_c) if dy == 0 else cut_y(dy, 1, deep, half_y, half_y, half_y, 2 * half_y)
                 moves.append((ODD, dx, dy, ref.at[pl.ds(src, count), ys], ref.at[pl.ds(dst, count), yd]))
         return moves
 
@@ -159,15 +166,18 @@
         corner = reach - 1
         low_c, high_c = (pl.ds(HX, corner), pl.ds(HX + rows, corner)), (pl.ds(HX + rows - corner, corner), pl.ds(HX - corner, corner))
         for dy in (-1, 1):
-            ys, yd = cut_y(dy, 1, corner, HY)
+            ys, yd = cut_y(dy, 1, corner)
             moves.append((ODD, 2, dy, ref.at[high_c[0], ys], ref.at[high_c[1], yd]))
             moves.append((ODD, -2, dy, ref.at[low_c[0], ys], ref.at[low_c[1], yd]))
         moves.append((ODD, 2, 0, ref.at[high[0], own_y], ref.at[high[1], own_y]))
         moves.append((ODD, -2, 0, ref.at[low[0], own_y], ref.at[low[1], own_y]))
         own_x = pl.ds(HX, rows)
         for dy in (-1, 1):
-            ys, yd = cut_y(dy, 1, reach, HY)
+            ys, yd = cut_y(dy, 1, HY)
             moves.append((ODD, 0, dy, ref.at[own_x, ys], ref.at[own_x, yd]))
+            if reach > HY:
+                y, j = fifth(dy)
+                moves.append((ODD, 0, dy, ref.at[own_x, y], fifth_p.at[:, j]))
         return moves
 
     def species_moves():
@@ -185,12 +195,12 @@
     sides = [
         (ODD, -1, 0, rim_v.at[0], out_x.at[0]),
         (ODD, -1, 0, rim_v.at[1], out_x.at[cells_x + 1]),
-        (ODD, -1, 0, rim_w.at[whole, 0], out_y.at[whole, HY - 1]),
-        (ODD, -1, 0, rim_w.at[whole, 1], out_y.at[whole, HY + cells_y]),
+        (ODD, -1, 0, rim_w.at[whole, 0], out_y.at[whole, wy - 1]),
+        (ODD, -1, 0, rim_w.at[whole, 1], out_y.at[whole, cells_y]),
     ]
 
-    f_x, g_x, m_x = exchange(first), exchange(rest), exchange(coarse_moves(coarse_m))
-    r_x = [exchange(coarse_moves(packed_r.at[at])) for at in range(CYCLES)]
+    f_x, g_x, m_x = exchange(first), exchange(rest), exchange(coarse_moves(coarse_m, OWN + 1, 7))
+    r_x = [exchange(coarse_moves(packed_r.at[at], OWN, 6)) for at in range(CYCLES)]
     p_x = [exchange(press_moves(press.at[at], HX - at)) for at in range(CYCLES)]
     s_x, b_x, v_x = exchange(species_moves()), exchange(back), exchange(sides)
     every = (f_x, g_x, m_x, *r_x, *p_x, s_x, b_x, v_x)
@@ -226,7 +236,7 @@
         copy.start()
     barrier = pltpu.get_barrier_semaphore()
     greet = {ODD: set(), EVEN: set()}
-    for moves in (first, rest, species_moves(), back):
+    for moves in (first, rest, coarse_moves(coarse_m, OWN + 1, 7), species_moves(), back):
         for by, dx, dy, _, _ in moves:
             greet[by].add((dx, dy))
             greet[(by + dx) % 2].add((-dx, -dy))
@@ -251,7 +261,7 @@
 
     @pl.when(odd)
     def _():
-        for ref in (near, later, edge_x, edge_y, coarse_m, packed_r, press, rim_x, rim_y):
+        for ref in (near, later, fifth_m, edge_x, edge_y, coarse_m, packed_r, press, fifth_p, rim_x, rim_y):
             ref[...] = jnp.zeros(ref.shape, f32)
         enter(ODD)
 
@@ -288,6 +298,7 @@
     @pl.when(jnp.logical_not(odd))
     def _():
         f_x[0](EVEN)
+        f_x[2](EVEN)
         g_x[0](EVEN)
         inputs[3].wait()
         s_x[0](EVEN)
@@ -296,21 +307,21 @@
             m = stage[0, x]
             p = given[1 + x, own_y]
             out_x[1 + x] = velocity[0, x] - m * (0.5 * (given[2 + x, own_y] - given[x, own_y]))
-            grad = given[1 + x, pl.ds(HY + 1, cells_y)] - given[1 + x, pl.ds(HY - 1, cells_y)]
-            out_y[x, own_y] = velocity[1, x] - m * (0.5 * grad)
+            v = given[1 + x]
+            out_y[x, own_y] = velocity[1, x] - m * (0.5 * (next_y(v) - prev_y(v))[:cells_y])
             row_o, lane_o = grids(cells_y)
             dz = jnp.where(lane_o == cells_z - 1, 0.0, next_z(p)) - jnp.where(lane_o == 0, 0.0, prev_z(p))
             out_z[x] = velocity[2, x] - m * (0.5 * dz)
             out_p[x] = p
         v_x[1](EVEN)
         s_x[1](EVEN)
-        for x in every:
+        for x in every[1:]:
             x[2](EVEN)
 
     @pl.when(odd)
     def _():
         f_x[0](ODD)
-        g_x[0](ODD)
+        f_x[2](ODD)
         row_w, lane_w = grids(wy)
         row_c, lane_c = grids(2 * half_y + half_y)
         even_c = lane_c % 2 == 0
@@ -320,9 +331,22 @@
         near[1, mine, own_y] = stage[1]
         edge_x[pl.ds(EDGES.index(cells_x), 2), own_y] = stage_x[...]
         edge_y[mine, pl.ds(1, 2)] = stage_y[:, pl.ds(1, 2)]
-        coarse_m[OWN + 1, own_c] = stage_c[...]
-        f_x[1](ODD)
+        coarse_m[OWN + 2, own_c] = stage_c[...]
+        f_x[1](ODD, True)
         m_x[0](ODD)
+        g_x[0](ODD)
+        f_x[1](ODD, False)
+
+        middle = grids(8)[0]
+
+        def around_y(v, more=None):
+            if more is None:
+                return prev_y(v), next_y(v)
+            own, rim = v[:cells_y], v[cells_y:]
+            return (
+                prev_y(jnp.concatenate([own, jnp.where(middle == 3, more, rim)], 0)),
+                next_y(jnp.concatenate([own, jnp.where(middle == 4, more, rim)], 0)),
+            )
 
         def fine_setup(span, full):
             def mob(x):
@@ -331,7 +355,8 @@
             for x in span:
                 m = mob(x)
                 lo_x, hi_x = m + mob(x - 1), m + mob(x + 1)
-                lo_y, hi_y = m + prev_y(m), m + next_y(m)
+                before, behind = around_y(m, fifth_m[x - HX] if full and HX <= x < HX + rows else None)
+                lo_y, hi_y = m + before, m + behind
                 lo_z = m + jnp.where(lane_w == 0, 0.0, prev_z(m))
                 hi_z = m + jnp.where(lane_w == cells_z - 1, 0.0, next_z(m))
                 diag = (lo_x + hi_x) + (lo_y + hi_y) + (lo_z + hi_z)
@@ -351,39 +376,36 @@
                 def side(j):
                     return jnp.broadcast_to(edge_y[x, pl.ds(j, 1)], t.shape)
 
-                t = t + jnp.where(row_w == HY - 1, side(1), 0.0) - jnp.where(row_w == HY, side(0), 0.0)
-                t = t + jnp.where(row_w == HY + cells_y - 1, side(3), 0.0)
-                t = t - jnp.where(row_w == HY + cells_y, side(2), 0.0)
+                t = t + jnp.where(row_w == wy - 1, side(1), 0.0) - jnp.where(row_w == 0, side(0), 0.0)
+                t = t + jnp.where(row_w == cells_y - 1, side(3), 0.0)
+                t = t - jnp.where(row_w == cells_y, side(2), 0.0)
                 b = t * (inv + inv)
                 goal[x] = b
                 if not full:
                     pa[x] = -b
                     if HX <= x < HX + rows:
-                        scale_back[x - HX] = (diag * (0.5 / damping))[HY : HY + cells_y]
+                        scale_back[x - HX] = (diag * (0.5 / damping))[:cells_y]
 
         fine_setup(range(HX - 2, HX + rows + 2), False)
 
-        def sweep(src, dst, low, high):
+        def sweep(src, dst, low, high, deep=False):
             for x in range(low, high):
                 v = src[x]
+                before, behind = around_y(v, fifth_p[x - HX] if deep and HX <= x < HX + rows else None)
                 t = xa[x] * src[x - 1] + xb[x] * src[x + 1]
-                t = t + (ya[x] * prev_y(v) + yb[x] * next_y(v))
+                t = t + (ya[x] * before + yb[x] * behind)
                 t = t + (za[x] * prev_z(v) + zb[x] * next_z(v))
                 dst[x] = (1.0 - damping) * v + (t - goal[x])
 
-        def beside(ref, low, high):
+        def beside(ref, low, high, last):
             up = {b: next_z(ref[b]) for b in range(max(low - 1, 0), high)}
-            down = {b: prev_z(ref[b]) for b in range(low, min(high + 1, blocks))}
+            down = {b: prev_z(ref[b]) for b in range(low, min(high + 1, last))}
             for b in range(low, high):
-                yield b, jnp.where(even_c, up[max(b - 1, 0)], down[b]), jnp.where(even_c, up[b], down[min(b + 1, blocks - 1)])
+                yield b, jnp.where(even_c, up[max(b - 1, 0)], down[b]), jnp.where(even_c, up[b], down[min(b + 1, last - 1)])
 
         def coarse_setup():
-            for b, lo, hi in beside(coarse_m, 0, blocks):
-                m = coarse_m[b]
-                if b == 0:
-                    lo = jnp.where(even_c, 0.0, lo)
-                if b == blocks - 1:
-                    hi = jnp.where(even_c, hi, 0.0)
+            for c, lo, hi in beside(coarse_m, 1, blocks + 1, blocks + 2):
+                m, b = coarse_m[c], c - 1
                 lo_x, hi_x = m + lo, m + hi
                 lo_y, hi_y = m + prev_y(m), m + next_y(m)
                 lo_z = m + jnp.where(lane_c < 2, 0.0, prev_z(m, 2))
@@ -398,14 +420,14 @@
                 cinv[b] = inv
 
         def coarse_sweep(src, dst, low, high):
-            for b, lo, hi in beside(src, low, high):
+            for b, lo, hi in beside(src, low, high, blocks):
                 v = src[b]
                 t = cxa[b] * lo + cxb[b] * hi
                 t = t + (cya[b] * prev_y(v) + cyb[b] * next_y(v))
                 t = t + (cza[b] * prev_z(v, 2) + czb[b] * next_z(v, 2))
                 dst[b] = (1.0 - damping) * v + (t - right[b])
 
-        def correct(at, pre, free, reach):
+        def correct(at, pre, free, reach, parts):
             press[at, pl.ds(HX, rows), own_y] = pre[pl.ds(HX, rows), own_y]
             for x in range(HX, HX + rows, 2):
                 total = None
@@ -414,7 +436,7 @@
                     t = xa[w] * pre[w - 1] + xb[w] * pre[w + 1]
                     t = t + (ya[w] * prev_y(v) + yb[w] * next_y(v))
                     t = t + (za[w] * prev_z(v) + zb[w] * next_z(v))
-                    d = (damping * v - (t - goal[w]))[HY : HY + cells_y] * scale_back[w - HX]
+                    d = (damping * v - (t - goal[w]))[:cells_y] * scale_back[w - HX]
                     total = d if total is None else total + d
                 fold[(x - HX) // 2] = total
             for b in range(2):
@@ -436,26 +458,37 @@
             coarse_sweep(ca, cb, 0, blocks)
             coarse_sweep(cb, ca, 1, blocks - 1)
             coarse_sweep(ca, cb, 1, blocks - 1)
-            margin = half_y - HY // 2
+            margin, tall = half_y - half_y // 2, 2 * cells_y
             for q in range(-3, rows // 2 + 3):
                 v = cb[OWN + q // 2]
                 v = jnp.where(even_c, v, prev_z(v)) if q % 2 == 0 else jnp.where(even_c, next_z(v), v)
-                v = v[margin : margin + wy // 2]
-                spread[q + 3, pl.ds(0, wy // 2, stride=2)] = v
-                spread[q + 3, pl.ds(1, wy // 2, stride=2)] = v
+                v = v[margin : margin + cells_y]
+                spread[q + 3, pl.ds(0, tall // 2, stride=2)] = v
+                spread[q + 3, pl.ds(1, tall // 2, stride=2)] = v
             p_x[at][1](ODD)
-            low, high = HX - reach - 2, HX + rows + reach + 2
-            for x in range(low, high):
-                pre[x] = press[at, x] + spread[(x - HX) // 2 + 3]
-            sweep(pre, free, low + 1, high - 1)
-            sweep(free, pre, low + 2, high - 2)
+            low, high = HX - reach, HX + rows + reach
+            done = [low - 2, low - 1, low]
+            for end in parts:
+                tops = [min(HX + end + 2, high + 2), min(HX + end + 1, high + 1), min(HX + end, high)]
+                for x in range(done[0], tops[0]):
+                    up = spread.at[(x - HX) // 2 + 3]
+                    ahead, after = up[pl.ds(0, 8)], up[pl.ds(8 + cells_y, 8)]
+                    pre[x, own_y] = press[at, x, own_y] + up[pl.ds(8, cells_y)]
+                    pre[x, pl.ds(cells_y, 8)] = press[at, x, pl.ds(cells_y, 8)] + jnp.where(middle < HY, after, ahead)
+                    if at == 0 and HX <= x < HX + rows:
+                        fifth_p[x - HX] = fifth_p[x - HX] + jnp.where(middle < HY, ahead, after)
+                sweep(pre, free, done[1], tops[1], at == 0)
+                sweep(free, pre, done[2], tops[2])
+                done = tops
+                yield
 
         sweep(pa, pb, HX - 1, HX + rows + 1)
-        correct(0, pb, pa, 3)
+        list(correct(0, pb, pa, 3, (rows + 3,)))
         sweep(pb, pa, HX - 2, HX + rows + 2)
         sweep(pa, pb, HX - 1, HX + rows + 1)
-        correct(1, pb, pa, 2)
         last = pb
+        finish = correct(1, pb, pa, 2, (cells_x + 2, rows + 2))
+        next(finish)
         b_x[0](ODD)
 
         def along_x(x):
@@ -463,7 +496,7 @@
 
         def along_y(x, y):
             one = pl.ds(y, 1)
-            return near[0, x, one] * (0.5 * (last[x, pl.ds(y + 1, 1)] - last[x, pl.ds(y - 1, 1)]))
+            return near[0, x, one] * (0.5 * (last[x, pl.ds((y + 1) % wy, 1)] - last[x, pl.ds(y - 1, 1)]))
 
         def edge(at):
             v = edge_x[EDGES.index(at), own_y]
@@ -471,7 +504,7 @@
 
         def ends(x):
             lo, hi = edge_y[x, pl.ds(0, 1)], edge_y[x, pl.ds(3, 1)]
-            return (lo + lo) - along_y(x, HY - 1), (hi + hi) - along_y(x, HY + cells_y)
+            return (lo + lo) - along_y(x, wy - 1), (hi + hi) - along_y(x, cells_y)
 
         rim_v[0] = edge(-1)
         rim_v[1] = edge(cells_x)
@@ -480,6 +513,7 @@
             rim_w[x, pl.ds(0, 1)] = lo
             rim_w[x, pl.ds(1, 1)] = hi
         v_x[0](ODD)
+        next(finish)
         out_x[0] = edge(cells_x - 1)
         out_x[cells_x + 1] = edge(rows)
         for x in range(cells_x):
@@ -487,22 +521,22 @@
             m = near[0, w, own_y]
             p = last[w, own_y]
             out_x[1 + x] = velocity[0, x] - along_x(w)
-            grad = last[w, pl.ds(HY + 1, cells_y)] - last[w, pl.ds(HY - 1, cells_y)]
-            out_y[x, own_y] = velocity[1, x] - m * (0.5 * grad)
+            v = last[w]
+            out_y[x, own_y] = velocity[1, x] - m * (0.5 * (next_y(v) - prev_y(v))[:cells_y])
             lo, hi = ends(w)
-            out_y[x, pl.ds(HY - 1, 1)] = lo
-            out_y[x, pl.ds(HY + cells_y, 1)] = hi
+            out_y[x, pl.ds(wy - 1, 1)] = lo
+            out_y[x, pl.ds(cells_y, 1)] = hi
             dz = jnp.where(lane_o == cells_z - 1, 0.0, next_z(p)) - jnp.where(lane_o == 0, 0.0, prev_z(p))
             out_z[x] = velocity[2, x] - m * (0.5 * dz)
             out_p[x] = p
         s_x[1](ODD)
-        for x in every:
+        for x in every[1:]:
             x[2](ODD)
 
     assert groups == MOVES, groups
 
 
-MOVES = [34, 18, 14, 14, 14, 8, 8, 8, 1, 4]
+MOVES = [34, 22, 14, 14, 14, 10, 8, 8, 1, 4]
 
 
 def transport(in_x, in_y, in_z, in_p, rim_x, rim_y, species, vel_out, pres_out, spec_out):
@@ -522,7 +556,7 @@
     def prev_y(v):
         return pltpu.roll(v, 1, 0)
 
-    mid = slice(HY, HY + cells_y)
+    mid = slice(0, cells_y)
     pres_out[...] = in_p[...]
     move_x = [in_x[x] for x in range(cells_x + 2)]
     for x in range(cells_x):
@@ -558,7 +592,7 @@
 
 def local(slabs, crosses, velocity, density, source, species):
     cells_x, cells_y, cells_z = density.shape
-    assert cells_x == 4 and cells_y == 2 * HY and slabs % 2 == 0
+    assert cells_x == 4 and cells_y == 16 and slabs % 2 == 0
     rows = 2 * cells_x
     wx, wy = rows + 2 * HX, cells_y + 2 * HY
     half_y = cells_y // 2
@@ -584,10 +618,10 @@
         out_specs=(spec,) * 7,
         scratch_shapes=[vmem(*velocity.shape), vmem(*density.shape), vmem(*density.shape)]
         + [vmem(2, *density.shape), vmem(2, cells_y, cells_z), vmem(cells_x, 8, cells_z), vmem(half_y, cells_z)]
-        + [vmem(2, *fine)] * 2 + [vmem(len(EDGES), wy, cells_z), vmem(wx, 8, cells_z)]
-        + [vmem(CYCLES, *fine), vmem(*coarse), vmem(CYCLES, *coarse), vmem(cells_x + 2, wy, cells_z)]
+        + [vmem(2, *fine)] * 2 + [vmem(rows, 8, cells_z), vmem(len(EDGES), wy, cells_z), vmem(wx, 8, cells_z)]
+        + [vmem(CYCLES, *fine), vmem(rows, 8, cells_z), vmem(blocks + 2, *coarse[1:]), vmem(CYCLES, *coarse), vmem(cells_x + 2, wy, cells_z)]
         + [vmem(*fine)] * 7 + [vmem(rows, cells_y, cells_z)] + [vmem(*fine)] * 2
-        + [vmem(*coarse)] * 10 + [vmem(cells_x, cells_y, cells_z), vmem(rows // 2 + 6, wy, cells_z)]
+        + [vmem(*coarse)] * 10 + [vmem(cells_x, cells_y, cells_z), vmem(rows // 2 + 6, 2 * cells_y, cells_z)]
         + [vmem(2, cells_y, cells_z), vmem(cells_x, 8, cells_z)]
         + [dma((4,))] + [dma((n,)) for n in MOVES for _ in range(2)],
         compiler_params=pltpu.CompilerParams(

time: 22.7 us -> 21.8 us (0.960)
  Pallas kernels: 21.9 us -> 21 us
    pallas_call x1, Pallas kernels: 20.9 us -> 20 us  [local(): pl.pallas_call(functools.partial(kernel, slabs, crosses), out_shape=tuple...]
where the time goes in v4:
time: 21.8 us; the launch traced here: 21.7 us
  Pallas kernels  21 us (96%)
  between operations  0.64 us (3%)
    pallas_call x1, Pallas kernels, local(): pl.pallas_call(functools.partial(kernel, slabs, crosses), out_shape=tuple...  20 us
    pallas_call x1, Pallas kernels, local(): pl.pallas_call(transport, out_shape=tuple((jax.ShapeDtypeStruct(a.shape,...  1.03 us

profile of v4, /device:TPU:0, one launch (start us, length us, event | category | flops | bytes accessed | tf_op | source)
XLA Modules:
  0.0 21.7 jit_solution(9665368296918462788)
XLA Ops:
  0.6 20.0 %projection.1 = (f32[6,16,128]{2,1,0:T(8,128)S(1)}, f32[4,24,128]{2,1,0:T(8,128)S(1)}, f32[4,16,128]{2,1,0:T(8,128)S(1)}, f32[4,16,128]{2,1,0:T(8,128)S(1)}, f32...) custom-call(f32[3,4,16,128]{3,2,1,0:T(8,128)} %velocity_in.1, ...), custom_call_target="tpu_custom_call" | custom-call | tf_op jit(solution)/shard_map/projection/pallas_call | solution.py:614
  20.6 1.0 %transport.1 = (f32[3,4,16,128]{3,2,1,0:T(8,128)}, f32[4,16,128]{2,1,0:T(8,128)}, f32[9,4,16,128]{3,2,1,0:T(8,128)}) custom-call(f32[6,16,128]{2,1,0:T(8,128)S(1)} %get-tuple-element.10.in_x, f32[4,24,128]{2,1,0:T(8,128)S(1)} %get-tuple-element.11.in_y, f32[4,16,128]{2,1,0:T(8,128)S(1)} %get-tuple-element.12.in_z, f32[4,16,128]{2,1,0:T(8,128)S(1)} %get-tuple-element.13.in_p, ...), custom_call_target="tpu_custom_call" | custom-call | tf_op jit(solution)/shard_map/transport/pallas_call | solution.py:632

commit v5 on v4

--- a/solution.py
+++ b/solution.py
@@ -27,8 +27,8 @@
     out_x, out_y, out_z, out_p, rim_x, rim_y, kinds,
     velocity, density, source, stage, stage_x, stage_y, stage_c,
     near, later, fifth_m, edge_x, edge_y, press, fifth_p, coarse_m, packed_r, given,
-    xa, xb, ya, yb, za, zb, goal, scale_back, pa, pb,
-    cxa, cxb, cya, cyb, cza, czb, cinv, right, ca, cb, fold, spread, rim_v, rim_w, in_sem, *sems,
+    xa, xb, ya, yb, za, zb, goal, scale_back, pb,
+    cxa, cxb, cya, cyb, cza, czb, cinv, right, fold, spread, rim_v, rim_w, in_sem, *sems,
 ):
     cells_x, cells_y, cells_z = density.shape
     rows = 2 * cells_x
@@ -113,7 +113,9 @@
             first.append((by, out, dy, stage_x.at[min(touch, 1), ys], edge_x.at[edge, yd]))
             first.append((by, out, dy, stage_y.at[whole, j], edge_y.at[pl.ds(HX + at, cells_x), k]))
         src, dst = seen(1, 3)
-        first.append((by, out, 0, stage.at[whole, src], near.at[whole, dst, own_y]))
+        first.append((by, out, 0, stage.at[0, src], near.at[0, dst, own_y]))
+        src, dst = seen(1, 2)
+        first.append((by, out, 0, stage.at[1, src], near.at[1, dst, own_y]))
         first.append((by, out, 0, stage_x.at[min(touch, 1)], edge_x.at[edge, own_y]))
         first.append((by, out, 0, stage_y.at[whole, pl.ds(1, 2)], edge_y.at[pl.ds(HX + at, cells_x), pl.ds(1, 2)]))
         mine = pl.ds(HX + base, cells_x)
@@ -136,7 +138,9 @@
                 ys, yd = cut_y(dy, low, high)
                 rest.append((by, out, dy, stage.at[whole, src, ys], later.at[whole, dst, yd]))
         src, dst = seen(4, 1)
-        rest.append((by, out, 0, stage.at[whole, src], later.at[whole, dst, own_y]))
+        rest.append((by, out, 0, stage.at[0, src], later.at[0, dst, own_y]))
+        src, dst = seen(3, 2)
+        rest.append((by, out, 0, stage.at[1, src], later.at[1, dst, own_y]))
         far, row, lands = (3, cells_x - 1, -HX) if by == EVEN else (-2, 0, rows + HX - 1)
         rest.append((by, far, 0, stage.at[0, row], later.at[0, HX + lands, own_y]))
         rest.append((by, far, 0, stage_x.at[min(row, 1)], edge_x.at[EDGES.index(lands), own_y]))
@@ -222,9 +226,13 @@
     def prev_y(v):
         return pltpu.roll(v, 1, 0)
 
+    def swap_z(v):
+        lane = grids(v.shape[0])[1]
+        return jnp.take_along_axis(v, lane + 1 - 2 * (lane % 2), axis=1)
+
     def pack(two):
         lane = grids(two[0].shape[0])[1]
-        return jnp.where(lane % 2 == 0, two[0] + next_z(two[0]), two[1] + prev_z(two[1]))
+        return jnp.where(lane % 2 == 0, two[0] + swap_z(two[0]), two[1] + swap_z(two[1]))
 
     inputs = [
         pltpu.make_async_copy(src, dst, in_sem.at[at])
@@ -242,7 +250,7 @@
             greet[(by + dx) % 2].add((-dx, -dy))
 
     def enter(role):
-        for dx, dy in sorted(greet[role], key=lambda d: (-abs(d[0]) - 2 * abs(d[1]), d)):
+        for dx, dy in sorted(greet[role], key=lambda d: (abs(d[0]) == 4, -abs(d[0]) - 2 * abs(d[1]), d)):
             @pl.when(there(dx, dy))
             def _():
                 pl.semaphore_signal(barrier, inc=1, device_id=(slab + dx, cross + dy), device_id_type=MESH)
@@ -381,30 +389,37 @@
                 t = t - jnp.where(row_w == cells_y, side(2), 0.0)
                 b = t * (inv + inv)
                 goal[x] = b
-                if not full:
-                    pa[x] = -b
-                    if HX <= x < HX + rows:
-                        scale_back[x - HX] = (diag * (0.5 / damping))[:cells_y]
-
-        fine_setup(range(HX - 2, HX + rows + 2), False)
-
-        def sweep(src, dst, low, high, deep=False):
-            for x in range(low, high):
-                v = src[x]
-                before, behind = around_y(v, fifth_p[x - HX] if deep and HX <= x < HX + rows else None)
-                t = xa[x] * src[x - 1] + xb[x] * src[x + 1]
-                t = t + (ya[x] * before + yb[x] * behind)
-                t = t + (za[x] * prev_z(v) + zb[x] * next_z(v))
-                dst[x] = (1.0 - damping) * v + (t - goal[x])
-
-        def beside(ref, low, high, last):
-            up = {b: next_z(ref[b]) for b in range(max(low - 1, 0), high)}
-            down = {b: prev_z(ref[b]) for b in range(low, min(high + 1, last))}
-            for b in range(low, high):
-                yield b, jnp.where(even_c, up[max(b - 1, 0)], down[b]), jnp.where(even_c, up[b], down[min(b + 1, last - 1)])
+                if not full and HX <= x < HX + rows:
+                    scale_back[x - HX] = (diag * (0.5 / damping))[:cells_y]
+            return -b
+
+        def faces(x, rows_of, more=None):
+            v = rows_of[x]
+            before, behind = around_y(v, more)
+            t = xa[x] * rows_of[x - 1] + xb[x] * rows_of[x + 1]
+            t = t + (ya[x] * before + yb[x] * behind)
+            return v, t + (za[x] * prev_z(v) + zb[x] * next_z(v))
+
+        def relax(x, rows_of, more=None):
+            v, t = faces(x, rows_of, more)
+            return (1.0 - damping) * v + (t - goal[x])
+
+        def cascade(levels, lag, rows_of=None, part=None):
+            if rows_of is None:
+                rows_of = [{} for _ in levels]
+            low = min(level[0] for level in levels)
+            high = max(level[1] for level in levels)
+            for step in range(low, high + lag * len(levels)):
+                for k, (start, end, row) in enumerate(levels):
+                    x = step - lag * k
+                    if start <= x < end and x not in rows_of[k] and (part is None or x < part[k]):
+                        rows_of[k][x] = row(x, rows_of[k - 1])
+            return rows_of
 
         def coarse_setup():
-            for c, lo, hi in beside(coarse_m, 1, blocks + 1, blocks + 2):
+            swapped = [swap_z(coarse_m[c]) for c in range(blocks + 2)]
+            for c in range(1, blocks + 1):
+                lo, hi = jnp.where(even_c, swapped[c - 1], swapped[c]), jnp.where(even_c, swapped[c], swapped[c + 1])
                 m, b = coarse_m[c], c - 1
                 lo_x, hi_x = m + lo, m + hi
                 lo_y, hi_y = m + prev_y(m), m + next_y(m)
@@ -419,76 +434,131 @@
                 czb[b] = jnp.where(lane_c >= cells_z - 2, 0.0, hi_z * inv)
                 cinv[b] = inv
 
-        def coarse_sweep(src, dst, low, high):
-            for b, lo, hi in beside(src, low, high, blocks):
-                v = src[b]
-                t = cxa[b] * lo + cxb[b] * hi
-                t = t + (cya[b] * prev_y(v) + cyb[b] * next_y(v))
-                t = t + (cza[b] * prev_z(v, 2) + czb[b] * next_z(v, 2))
-                dst[b] = (1.0 - damping) * v + (t - right[b])
-
-        def correct(at, pre, free, reach, parts):
-            press[at, pl.ds(HX, rows), own_y] = pre[pl.ds(HX, rows), own_y]
-            for x in range(HX, HX + rows, 2):
-                total = None
-                for w in (x, x + 1):
-                    v = pre[w]
-                    t = xa[w] * pre[w - 1] + xb[w] * pre[w + 1]
-                    t = t + (ya[w] * prev_y(v) + yb[w] * next_y(v))
-                    t = t + (za[w] * prev_z(v) + zb[w] * next_z(v))
-                    d = (damping * v - (t - goal[w]))[:cells_y] * scale_back[w - HX]
-                    total = d if total is None else total + d
-                fold[(x - HX) // 2] = total
+        shifted = {}
+
+        def swapped(rows_of, b):
+            key = (id(rows_of), b)
+            if key not in shifted:
+                shifted[key] = swap_z(rows_of[b])
+            return shifted[key]
+
+        def coarse_relax(b, rows_of):
+            v = rows_of[b]
+            before = b - 1 if b - 1 in rows_of else b
+            behind = b + 1 if b + 1 in rows_of else b
+            lo = jnp.where(even_c, swapped(rows_of, before), swapped(rows_of, b))
+            hi = jnp.where(even_c, swapped(rows_of, b), swapped(rows_of, behind))
+            t = cxa[b] * lo + cxb[b] * hi
+            t = t + (cya[b] * prev_y(v) + cyb[b] * next_y(v))
+            t = t + (cza[b] * prev_z(v, 2) + czb[b] * next_z(v, 2))
+            return (1.0 - damping) * v + (t - right[b])
+
+        own = range(HX, HX + rows)
+        margin, tall = half_y // 2, 2 * cells_y
+
+        def send(at, deeper):
+            totals = {}
+
+            def smoothed(x, rows_of):
+                v = deeper(x, rows_of)
+                if x in own:
+                    press[at, x, own_y] = v[:cells_y]
+                return v
+
+            def residual(x, rows_of):
+                v, t = faces(x, rows_of)
+                d = (damping * v - (t - goal[x]))[:cells_y] * scale_back[x - HX]
+                totals[x] = d
+                if (x - HX) % 2 == 1:
+                    fold[(x - HX) // 2] = totals[x - 1] + d
+                return d
+
+            return smoothed, residual
+
+        def leave_off(at):
             for b in range(2):
                 packed_r[at, OWN + b, own_c] = pack([folded(2 * b), folded(2 * b + 1)])
             r_x[at][0](ODD)
             p_x[at][0](ODD)
-            if at == 0:
-                inputs[3].wait()
-                s_x[0](ODD)
-                g_x[1](ODD)
-                fine_setup(range(1, wx - 1), True)
-                m_x[1](ODD)
-                coarse_setup()
+
+        def correct(at):
             r_x[at][1](ODD)
-            for b in range(blocks):
+
+            def begin(b, _):
                 r = packed_r[at, b] * cinv[b]
                 right[b] = r
-                ca[b] = -r
-            coarse_sweep(ca, cb, 0, blocks)
-            coarse_sweep(cb, ca, 1, blocks - 1)
-            coarse_sweep(ca, cb, 1, blocks - 1)
-            margin, tall = half_y - half_y // 2, 2 * cells_y
-            for q in range(-3, rows // 2 + 3):
-                v = cb[OWN + q // 2]
-                v = jnp.where(even_c, v, prev_z(v)) if q % 2 == 0 else jnp.where(even_c, next_z(v), v)
-                v = v[margin : margin + cells_y]
-                spread[q + 3, pl.ds(0, tall // 2, stride=2)] = v
-                spread[q + 3, pl.ds(1, tall // 2, stride=2)] = v
+                return -r
+
+            def prolong(b, rows_of):
+                c = coarse_relax(b, rows_of)
+                d = swap_z(c)
+                for odd_row in (0, 1):
+                    q = 2 * (b - OWN) + odd_row
+                    if -3 <= q < rows // 2 + 3:
+                        v = jnp.where(even_c, d, c) if odd_row else jnp.where(even_c, c, d)
+                        v = v[margin : margin + cells_y]
+                        spread[q + 3, pl.ds(0, tall // 2, stride=2)] = v
+                        spread[q + 3, pl.ds(1, tall // 2, stride=2)] = v
+                return c
+
+            held = [(0, blocks, begin), (0, blocks, coarse_relax), (1, blocks - 1, coarse_relax), (1, blocks - 1, prolong)]
+            kept = cascade(held, 20)
+            shifted.clear()
             p_x[at][1](ODD)
-            low, high = HX - reach, HX + rows + reach
-            done = [low - 2, low - 1, low]
-            for end in parts:
-                tops = [min(HX + end + 2, high + 2), min(HX + end + 1, high + 1), min(HX + end, high)]
-                for x in range(done[0], tops[0]):
-                    up = spread.at[(x - HX) // 2 + 3]
-                    ahead, after = up[pl.ds(0, 8)], up[pl.ds(8 + cells_y, 8)]
-                    pre[x, own_y] = press[at, x, own_y] + up[pl.ds(8, cells_y)]
-                    pre[x, pl.ds(cells_y, 8)] = press[at, x, pl.ds(cells_y, 8)] + jnp.where(middle < HY, after, ahead)
-                    if at == 0 and HX <= x < HX + rows:
-                        fifth_p[x - HX] = fifth_p[x - HX] + jnp.where(middle < HY, ahead, after)
-                sweep(pre, free, done[1], tops[1], at == 0)
-                sweep(free, pre, done[2], tops[2])
-                done = tops
-                yield
-
-        sweep(pa, pb, HX - 1, HX + rows + 1)
-        list(correct(0, pb, pa, 3, (rows + 3,)))
-        sweep(pb, pa, HX - 2, HX + rows + 2)
-        sweep(pa, pb, HX - 1, HX + rows + 1)
+            fifths = {}
+
+            def add(x, _):
+                up = spread.at[(x - HX) // 2 + 3]
+                ahead, after = up[pl.ds(0, 8)], up[pl.ds(8 + cells_y, 8)]
+                if at == 0 and x in own:
+                    fifths[x] = fifth_p[x - HX] + jnp.where(middle < HY, ahead, after)
+                change = jnp.concatenate([up[pl.ds(8, cells_y)], jnp.where(middle < HY, after, ahead)], 0)
+                return press[at, x] + change
+
+            return add, lambda x, rows_of: relax(x, rows_of, fifths.get(x))
+
+        low, high = HX, HX + rows
+        smoothed, residual = send(0, relax)
+        cascade(
+            [
+                (low - 2, high + 2, lambda x, _: fine_setup((x,), False)),
+                (low - 1, high + 1, smoothed),
+                (low, high, residual),
+            ],
+            20,
+        )
+        leave_off(0)
+        inputs[3].wait()
+        s_x[0](ODD)
+        g_x[1](ODD)
+        fine_setup(range(1, wx - 1), True)
+        m_x[1](ODD)
+        coarse_setup()
+        add, first_relax = correct(0)
+        smoothed, residual = send(1, relax)
+        cascade(
+            [
+                (low - 5, high + 5, add),
+                (low - 4, high + 4, first_relax),
+                (low - 3, high + 3, relax),
+                (low - 2, high + 2, relax),
+                (low - 1, high + 1, smoothed),
+                (low, high, residual),
+            ],
+            20,
+        )
+        leave_off(1)
         last = pb
-        finish = correct(1, pb, pa, 2, (cells_x + 2, rows + 2))
-        next(finish)
+        add, first_relax = correct(1)
+
+        def final(x, rows_of):
+            v = relax(x, rows_of)
+            last[x] = v
+            return v
+
+        levels = [(low - 4, high + 4, add), (low - 3, high + 3, first_relax), (low - 2, high + 2, final)]
+        top = HX + cells_x + 2
+        kept = cascade(levels, 20, None, (top + 2, top + 1, top))
         b_x[0](ODD)
 
         def along_x(x):
@@ -513,7 +583,7 @@
             rim_w[x, pl.ds(0, 1)] = lo
             rim_w[x, pl.ds(1, 1)] = hi
         v_x[0](ODD)
-        next(finish)
+        cascade(levels, 20, kept)
         out_x[0] = edge(cells_x - 1)
         out_x[cells_x + 1] = edge(rows)
         for x in range(cells_x):
@@ -536,10 +606,10 @@
     assert groups == MOVES, groups
 
 
-MOVES = [34, 22, 14, 14, 14, 10, 8, 8, 1, 4]
-
-
-def transport(in_x, in_y, in_z, in_p, rim_x, rim_y, species, vel_out, pres_out, spec_out):
+MOVES = [36, 24, 14, 14, 14, 10, 8, 8, 1, 4]
+
+
+def transport(in_x, in_y, in_z, in_p, rim_x, rim_y, species, vel_out, pres_out, spec_out, stage, sems):
     cells_x, cells_y, cells_z = in_p.shape
     lane_o = lax.broadcasted_iota(jnp.int32, (cells_y, cells_z), 1)
     row_o = lax.broadcasted_iota(jnp.int32, (cells_y, cells_z), 0)
@@ -557,13 +627,23 @@
         return pltpu.roll(v, 1, 0)
 
     mid = slice(0, cells_y)
-    pres_out[...] = in_p[...]
+    copies = [
+        pltpu.make_async_copy(src, dst, sems.at[at])
+        for at, (src, dst) in enumerate(
+            (
+                (in_x.at[pl.ds(1, cells_x)], vel_out.at[0]),
+                (in_y.at[:, pl.ds(0, cells_y)], vel_out.at[1]),
+                (in_z, vel_out.at[2]),
+                (in_p, pres_out),
+                *((stage.at[x], spec_out.at[:, x]) for x in range(cells_x)),
+            )
+        )
+    ]
+    for copy in copies[:4]:
+        copy.start()
     move_x = [in_x[x] for x in range(cells_x + 2)]
     for x in range(cells_x):
         move_y, move_z = in_y[x], in_z[x]
-        vel_out[0, x] = move_x[x + 1]
-        vel_out[1, x] = move_y[mid]
-        vel_out[2, x] = move_z
         lo_x, hi_x = 0.5 * (move_x[x] + move_x[x + 1]), 0.5 * (move_x[x + 1] + move_x[x + 2])
         lo_y, hi_y = (0.5 * (move_y + prev_y(move_y)))[mid], (0.5 * (move_y + next_y(move_y)))[mid]
         lo_z = 0.5 * (move_z + jnp.where(lane_o == 0, 0.0, prev_z(move_z)))
@@ -587,7 +667,10 @@
             yl = jnp.where(row_o == 0, rim_y[0, s, pl.ds(x, 1)], prev_y(q))
             yu = jnp.where(row_o == cells_y - 1, rim_y[1, s, pl.ds(x, 1)], next_y(q))
             total = keep * q + (from_xl * xl + from_xu * xu) + (from_yl * yl + from_yu * yu)
-            spec_out[s, x] = total + (from_zl * prev_z(q) + from_zu * next_z(q))
+            stage[x, s] = total + (from_zl * prev_z(q) + from_zu * next_z(q))
+        copies[4 + x].start()
+    for copy in copies:
+        copy.wait()
 
 
 def local(slabs, crosses, velocity, density, source, species):
@@ -620,8 +703,8 @@
         + [vmem(2, *density.shape), vmem(2, cells_y, cells_z), vmem(cells_x, 8, cells_z), vmem(half_y, cells_z)]
         + [vmem(2, *fine)] * 2 + [vmem(rows, 8, cells_z), vmem(len(EDGES), wy, cells_z), vmem(wx, 8, cells_z)]
         + [vmem(CYCLES, *fine), vmem(rows, 8, cells_z), vmem(blocks + 2, *coarse[1:]), vmem(CYCLES, *coarse), vmem(cells_x + 2, wy, cells_z)]
-        + [vmem(*fine)] * 7 + [vmem(rows, cells_y, cells_z)] + [vmem(*fine)] * 2
-        + [vmem(*coarse)] * 10 + [vmem(cells_x, cells_y, cells_z), vmem(rows // 2 + 6, 2 * cells_y, cells_z)]
+        + [vmem(*fine)] * 7 + [vmem(rows, cells_y, cells_z), vmem(*fine)]
+        + [vmem(*coarse)] * 8 + [vmem(cells_x, cells_y, cells_z), vmem(rows // 2 + 6, 2 * cells_y, cells_z)]
         + [vmem(2, cells_y, cells_z), vmem(cells_x, 8, cells_z)]
         + [dma((4,))] + [dma((n,)) for n in MOVES for _ in range(2)],
         compiler_params=pltpu.CompilerParams(
@@ -633,7 +716,8 @@
         transport,
         out_shape=tuple(jax.ShapeDtypeStruct(a.shape, f32) for a in (velocity, density, species)),
         in_specs=[spec] * 7,
-        out_specs=(spec,) * 3,
+        out_specs=(far,) * 3,
+        scratch_shapes=[vmem(cells_x, kinds, cells_y, cells_z), dma((4 + cells_x,))],
         compiler_params=pltpu.CompilerParams(vmem_limit_bytes=8 << 20),
         name="transport",
     )(*between)

time: 21.8 us -> 21.6 us (level)
    pallas_call x1, Pallas kernels: 20 us -> 19.8 us  [local(): pl.pallas_call(functools.partial(kernel, slabs, crosses), out_shape=tuple...]
where the time goes in v5:
time: 21.6 us; the launch traced here: 21.4 us
  Pallas kernels  20.8 us (96%)
  between operations  0.64 us (3%)
    pallas_call x1, Pallas kernels, local(): pl.pallas_call(functools.partial(kernel, slabs, crosses), out_shape=tuple...  19.8 us
    pallas_call x1, Pallas kernels, local(): pl.pallas_call(transport, out_shape=tuple((jax.ShapeDtypeStruct(a.shape,...  1.01 us

profile of v5, /device:TPU:0, one launch (start us, length us, event | category | flops | bytes accessed | tf_op | source)
XLA Modules:
  0.0 21.4 jit_solution(15165000943247572205)
XLA Ops:
  0.6 19.8 %projection.1 = (f32[6,16,128]{2,1,0:T(8,128)S(1)}, f32[4,24,128]{2,1,0:T(8,128)S(1)}, f32[4,16,128]{2,1,0:T(8,128)S(1)}, f32[4,16,128]{2,1,0:T(8,128)S(1)}, f32...) custom-call(f32[3,4,16,128]{3,2,1,0:T(8,128)} %velocity_in.1, ...), custom_call_target="tpu_custom_call" | custom-call | tf_op jit(solution)/shard_map/projection/pallas_call | solution.py:697
  20.4 1.0 %transport.1 = (f32[3,4,16,128]{3,2,1,0:T(8,128)}, f32[4,16,128]{2,1,0:T(8,128)}, f32[9,4,16,128]{3,2,1,0:T(8,128)}) custom-call(f32[6,16,128]{2,1,0:T(8,128)S(1)} %get-tuple-element.10.in_x, f32[4,24,128]{2,1,0:T(8,128)S(1)} %get-tuple-element.11.in_y, f32[4,16,128]{2,1,0:T(8,128)S(1)} %get-tuple-element.12.in_z, f32[4,16,128]{2,1,0:T(8,128)S(1)} %get-tuple-element.13.in_p, ...), custom_call_target="tpu_custom_call" | custom-call | tf_op jit(solution)/shard_map/transport/pallas_call | solution.py:715
